TPU v7x, 768 devices: a whole 4x8x12 slice. The times are simulated.
768 devices in a mesh: ta: 192 (over x, y, z_lo, core), gz: 4 (over z_hi).
Axes of the slice: x: 4, y: 8, z: 12 (z_hi: 4, z_lo: 3; z = z_hi * 3 + z_lo), core: 2. Of those that a mesh axis runs over, the one named last changes fastest.
Arguments:
- spinor: float32 [2, 4, 3, 384, 8, 768], P(None, None, None, 'ta', 'gz'), may hold values from -3 to 3
- links: float32 [4, 2, 3, 3, 384, 8, 768], P(None, None, None, None, 'ta', 'gz'), may hold values from -3.5 to 3.5
- clover: float32 [2, 2, 6, 6, 384, 8, 768], P(None, None, None, None, 'ta', 'gz'), may hold values from -1.2 to 1.2
Outputs:
- applied: float32 [2, 4, 3, 384, 8, 768], P(None, None, None, 'ta', 'gz')
- force: float32 [4, 2, 3, 3, 384, 8, 768], P(None, None, None, None, 'ta', 'gz')
All inputs are finite; a program needn't handle non-finite values.
Results may differ from a plain program's by a relative error of at most 0.0001.
Values sent between devices are 32-bit elements; how exact they have to be, the bound alone decides.
No kernel may reach another device: no remote copies, remote signals or barrier semaphores. Data moves between devices by JAX's collectives and lax.ppermute only.
A program may use at most 64 MiB of HBM per device.

v0:
```python
import jax
import jax.numpy as jnp
from jax import lax
from jax.sharding import PartitionSpec as P

NY = 12
NX = 64


bare_mass = -0.25
gamma_table = (
    ((3, 0.0, -1.0), (2, 0.0, -1.0), (1, 0.0, 1.0), (0, 0.0, 1.0)),
    ((3, -1.0, 0.0), (2, 1.0, 0.0), (1, 1.0, 0.0), (0, -1.0, 0.0)),
    ((2, 0.0, -1.0), (3, 0.0, 1.0), (0, 0.0, 1.0), (1, 0.0, -1.0)),
    ((2, 1.0, 0.0), (3, 1.0, 0.0), (0, 1.0, 0.0), (1, 1.0, 0.0)),
)


def padded(shard, sides, width):
    edges = {}
    for axis, dim in sides:
        devices, length = (lax.axis_size(axis), shard.shape[dim])
        up = [(i, (i + 1) % devices) for i in range(devices)]
        last = lax.slice_in_dim(shard, length - width, length, axis=dim)
        leading = lax.slice_in_dim(shard, 0, width, axis=dim)
        edges[dim] = (
            lax.ppermute(last, axis, up),
            lax.ppermute(leading, axis, [(b, a) for a, b in up]),
        )
    done = []
    for _, dim in sides:
        low, high = edges[dim]
        around = [(width, width) if d in done else (0, 0) for d in range(shard.ndim)]
        shard = jnp.concatenate([jnp.pad(low, around), shard, jnp.pad(high, around)], axis=dim)
        done.append(dim)
    return shard


def passed_along(value, axis, steps):
    count = lax.axis_size(axis)
    pairs = [(source, (source + steps) % count) for source in range(count)]
    return lax.ppermute(value, axis, pairs)


def apply_gamma(hop_dir, field):
    parts_re = []
    parts_im = []
    for spin_row in range(4):
        source, phase_re, phase_im = gamma_table[hop_dir][spin_row]
        source_re = field[0, source]
        source_im = field[1, source]
        if phase_im == 0.0:
            parts_re.append(phase_re * source_re)
            parts_im.append(phase_re * source_im)
        else:
            parts_re.append(-phase_im * source_im)
            parts_im.append(phase_im * source_re)
    return jnp.stack([jnp.stack(parts_re), jnp.stack(parts_im)])


def project(hop_dir, field, sign):
    return field + sign * apply_gamma(hop_dir, field)


def color_apply(link, field, dagger):
    link_re = link[0]
    link_im = link[1]
    if dagger:
        link_re = jnp.swapaxes(link_re, 0, 1)
        link_im = -jnp.swapaxes(link_im, 0, 1)
    matrix_re = link_re[None]
    matrix_im = link_im[None]
    field_re = field[0][:, None]
    field_im = field[1][:, None]
    out_re = jnp.sum(matrix_re * field_re - matrix_im * field_im, axis=2)
    out_im = jnp.sum(matrix_re * field_im + matrix_im * field_re, axis=2)
    return jnp.stack([out_re, out_im])


def clover_apply(clover, field):
    halves = field.reshape((2, 2, 6) + field.shape[3:])
    field_re = halves[0][:, None]
    field_im = halves[1][:, None]
    out_re = jnp.sum(clover[0] * field_re - clover[1] * field_im, axis=2)
    out_im = jnp.sum(clover[0] * field_im + clover[1] * field_re, axis=2)
    return jnp.stack([out_re, out_im]).reshape(field.shape)


def spin_outer(left, right):
    left_re = left[0][:, :, None]
    left_im = left[1][:, :, None]
    right_re = right[0][:, None]
    right_im = right[1][:, None]
    out_re = jnp.sum(left_re * right_re + left_im * right_im, axis=0)
    out_im = jnp.sum(left_im * right_re - left_re * right_im, axis=0)
    return jnp.stack([out_re, out_im])


def color_product(first, second):
    first_re = first[0][:, :, None]
    first_im = first[1][:, :, None]
    second_re = second[0][None]
    second_im = second[1][None]
    out_re = jnp.sum(first_re * second_re - first_im * second_im, axis=1)
    out_im = jnp.sum(first_re * second_im + first_im * second_re, axis=1)
    return jnp.stack([out_re, out_im])


def traceless(matrix):
    mat_re = matrix[0]
    mat_im = matrix[1]
    anti_re = 0.5 * (mat_re - jnp.swapaxes(mat_re, 0, 1))
    anti_im = 0.5 * (mat_im + jnp.swapaxes(mat_im, 0, 1))
    trace_third = (mat_im[0, 0] + mat_im[1, 1] + mat_im[2, 2]) / 3.0
    identity = jnp.eye(3, dtype=jnp.float32).reshape((3, 3) + (1,) * (mat_re.ndim - 2))
    return jnp.stack([anti_re, anti_im - identity * trace_third])


def along_plane(field, hop_dir, step):
    shape = field.shape
    grid = field.reshape(shape[:-1] + (NY, NX))
    if hop_dir == 0:
        grid = jnp.roll(grid, -step, axis=-1)
    else:
        grid = jnp.roll(grid, -step, axis=-2)
    return grid.reshape(shape)


def slab(field, start, stop, dimension):
    return lax.slice_in_dim(field, start, stop, axis=dimension)


def body(spinor, links, clover):
    t_slices = spinor.shape[3]
    z_slices = spinor.shape[4]
    t_place = lax.axis_index("ta")
    t_count = lax.axis_size("ta")
    low_sign = jnp.where(t_place == 0, -1.0, 1.0).astype(jnp.float32)
    high_sign = jnp.where(t_place == t_count - 1, -1.0, 1.0).astype(jnp.float32)
    forward_half = []
    hopping = jnp.zeros_like(spinor)
    for hop_dir in (0, 1):
        ahead_proj = project(hop_dir, along_plane(spinor, hop_dir, 1), -1.0)
        forward_half.append(ahead_proj)
        behind = along_plane(spinor, hop_dir, -1)
        back_link = along_plane(links[hop_dir], hop_dir, -1)
        hopping = (
            hopping
            + color_apply(links[hop_dir], ahead_proj, False)
            + color_apply(back_link, project(hop_dir, behind, 1.0), True)
        )
    extended = padded(spinor, (("ta", 3), ("gz", 4)), 1)
    link_t_low = passed_along(links[3][:, :, :, t_slices - 1 :], "ta", 1)
    link_z_low = passed_along(links[2][:, :, :, :, z_slices - 1 :], "gz", 1)
    z_upper = extended[:, :, :, 1 : t_slices + 1, z_slices + 1 :]
    z_lower = extended[:, :, :, 1 : t_slices + 1, :1]
    t_upper = extended[:, :, :, t_slices + 1 :, 1 : z_slices + 1] * high_sign
    t_lower = extended[:, :, :, :1, 1 : z_slices + 1] * low_sign
    for hop_dir, dimension, upper_face, lower_face, link_face in (
        (2, 4, z_upper, z_lower, link_z_low),
        (3, 3, t_upper, t_lower, link_t_low),
    ):
        size_here = spinor.shape[dimension]
        ahead = jnp.concatenate([slab(spinor, 1, size_here, dimension), upper_face], axis=dimension)
        behind = jnp.concatenate(
            [lower_face, slab(spinor, 0, size_here - 1, dimension)], axis=dimension
        )
        back_link = jnp.concatenate(
            [link_face, slab(links[hop_dir], 0, size_here - 1, dimension)], axis=dimension
        )
        ahead_proj = project(hop_dir, ahead, -1.0)
        forward_half.append(ahead_proj)
        hopping = (
            hopping
            + color_apply(links[hop_dir], ahead_proj, False)
            + color_apply(back_link, project(hop_dir, behind, 1.0), True)
        )
    applied = (4.0 + bare_mass) * spinor + clover_apply(clover, spinor) - 0.5 * hopping
    applied_t = passed_along(applied[:, :, :, :1], "ta", -1) * high_sign
    applied_z = passed_along(applied[:, :, :, :, :1], "gz", -1)
    ahead_applied = [
        along_plane(applied, 0, 1),
        along_plane(applied, 1, 1),
        jnp.concatenate([applied[:, :, :, :, 1:], applied_z], axis=4),
        jnp.concatenate([applied[:, :, :, 1:], applied_t], axis=3),
    ]
    forces = []
    for hop_dir in range(4):
        summed = spin_outer(forward_half[hop_dir], applied) + spin_outer(
            project(hop_dir, ahead_applied[hop_dir], 1.0), spinor
        )
        forces.append(traceless(color_product(links[hop_dir], summed)))
    return (applied, jnp.stack(forces))


def solution(mesh):
    return jax.shard_map(
        body,
        mesh=mesh,
        in_specs=(
            P(None, None, None, "ta", "gz", None),
            P(None, None, None, None, "ta", "gz", None),
            P(None, None, None, None, "ta", "gz", None),
        ),
        out_specs=(
            P(None, None, None, "ta", "gz", None),
            P(None, None, None, None, "ta", "gz", None),
        ),
        check_vma=False,
    )
```

profile of v0, /device:TPU:1, one launch (start us, length us, event | category | flops | bytes accessed | tf_op | source)
XLA Modules:
  0.0 120.6 jit_solution(15375502235729507288)
XLA Ops:
  0.6 1.1 fusion.161
  1.7 0.7 copy.475
  2.4 12.5 %collective-permute-start.3 = (f32[2,4,3,1,2,768]{5,1,4,3,2,0:T(4,128)}, f32[2,4,3,1,2,768]{5,1,4,3,2,0:T(4,128)}, u32[]{:S(2)}, u32[]{:S(2)}) collective-permute-start(f32[2,4,3,1,2,768]{5,1,4,3,2,0:T(4,128)} %copy.475), channel_id=1, source_target_pairs={{4,0},{8,4},{12,8},{16,12},{20,16},{24,20},{28,24},{32,28},{36,32}... | collective-permute-start | bytes 442376 | tf_op jit(solution)/shard_map/ppermute | solution.py:28
  14.9 1.4 %fusion.162 = (f32[2,4,3,2,1,768]{5,4,3,2,1,0:T(1,128)S(1)}, f32[2,4,3,2,1,768]{5,4,3,2,1,0:T(1,128)S(1)}) fusion(f32[2,4,3,2,2,768]{5,4,3,2,1,0:T(2,128)} %param.3), kind=kLoop, calls=%fused_computation.519 | loop fusion | bytes 589824 | tf_op jit(solution)/shard_map/slice | solution.py:130
  17.0 5.3 %collective-permute-start = (f32[2,4,3,2,1,768]{5,1,4,3,2,0:T(4,128)}, f32[2,4,3,2,1,768]{5,1,4,3,2,0:T(4,128)}, u32[]{:S(2)}, u32[]{:S(2)}) collective-permute-start(f32[2,4,3,2,1,768]{5,1,4,3,2,0:T(4,128)} %copy.473), channel_id=1, source_target_pairs={{1,0},{2,1},{3,2},{0,3},{5,4},{6,5},{7,6},{4,7},{9,8},{10,9},{11,1... | collective-permute-start | bytes 442376 | tf_op jit(solution)/shard_map/ppermute | solution.py:28
  22.3 0.7 copy.474
  23.0 1.9 %collective-permute-start.2 = (f32[2,4,3,2,1,768]{5,1,4,3,2,0:T(4,128)}, f32[2,4,3,2,1,768]{5,1,4,3,2,0:T(4,128)}, u32[]{:S(2)}, u32[]{:S(2)}) collective-permute-start(f32[2,4,3,2,1,768]{5,1,4,3,2,0:T(4,128)} %copy.474), channel_id=1, source_target_pairs={{0,1},{1,2},{2,3},{3,0},{4,5},{5,6},{6,7},{7,4},{8,9},{9,10},{10,1... | collective-permute-start | bytes 442376 | tf_op jit(solution)/shard_map/ppermute | solution.py:27
  24.9 0.9 slice_bitcast_fusion
  25.8 0.9 fusion.166
  26.6 2.1 %collective-permute-start.1 = (f32[2,3,3,2,1,768]{5,4,3,2,1,0:T(1,128)}, f32[2,3,3,2,1,768]{5,4,3,2,1,0:T(1,128)}, u32[]{:S(2)}, u32[]{:S(2)}) collective-permute-start(f32[2,3,3,2,1,768]{5,4,3,2,1,0:T(1,128)} %get-tuple-element.232), channel_id=1, source_target_pairs={{0,1},{1,2},{2,3},{3,0},{4,5},{5,6},{6,7},{7,4},{8,9},{9,10},{10,1... | collective-permute-start | bytes 331784 | tf_op jit(solution)/shard_map/ppermute | solution.py:42
  29.5 4.2 %collective-permute-start.5 = (f32[2,4,3,1,2,768]{5,1,4,3,2,0:T(4,128)}, f32[2,4,3,1,2,768]{5,1,4,3,2,0:T(4,128)}, u32[]{:S(2)}, u32[]{:S(2)}) collective-permute-start(f32[2,4,3,1,2,768]{5,1,4,3,2,0:T(4,128)} %copy.476), channel_id=1, source_target_pairs={{0,4},{4,8},{8,12},{12,16},{16,20},{20,24},{24,28},{28,32},{32,36}... | collective-permute-start | bytes 442376 | tf_op jit(solution)/shard_map/ppermute | solution.py:27
  33.6 0.9 slice_bitcast_fusion.45
  35.5 0.9 slice_bitcast_fusion.37
  36.7 1.2 copy-done.3
  37.9 1.3 %fusion.1 = (f32[2,6,2,2,768]{4,3,2,1,0:T(2,128)S(1)}, f32[2,6,2,2,768]{4,3,2,1,0:T(2,128)S(1)}) fusion(f32[2,2,6,6,2,2,768]{6,5,4,3,2,1,0:T(2,128)S(1)} %copy-done.3, f32[2,6,2,2,768]{4,3,2,1,0:T(2,128)S(1)} %bitcast.686, f32[2,6,2,2,768]{4,3,2,1,0:T(2,128)S(1)} %bitcast.685), kind=kLoop, calls=%fused_computation.4 | loop fusion | flops 1695744 | bytes 2359296 | tf_op jit(solution)/shard_map/reduce_sum | solution.py:84
  39.2 0.7 copy.180
  41.1 1.1 reshape.579
  42.1 1.0 fusion.164
  44.0 0.7 slice_bitcast_fusion.27
  46.0 0.7 slice_bitcast_fusion.25
  47.4 0.8 squeeze.18
  48.2 0.8 neg.37
  51.9 0.7 slice_bitcast_fusion.21
  54.3 0.7 copy.268
  56.6 2.1 %collective-permute-start.4 = (f32[2,3,3,1,2,768]{5,4,3,2,1,0:T(2,128)S(1)}, f32[2,3,3,1,2,768]{5,4,3,2,1,0:T(2,128)S(1)}, u32[]{:S(2)}, u32[]{:S(2)}) collective-permute-start(f32[2,3,3,1,2,768]{5,4,3,2,1,0:T(2,128)S(1)} %get-tuple-element.228), channel_id=1, source_target_pairs={{0,4},{4,8},{8,12},{12,16},{16,20},{20,24},{24,28},{28,32},{32,36}... | collective-permute-start | bytes 331784 | tf_op jit(solution)/shard_map/ppermute | solution.py:42
  58.7 1.0 fusion.27
  59.8 5.6 %collective-permute-done.4 = f32[2,3,3,1,2,768]{5,4,3,2,1,0:T(2,128)S(1)} collective-permute-done((f32[2,3,3,1,2,768]{5,4,3,2,1,0:T(2,128)S(1)}, f32[2,3,3,1,2,768]{5,4,3,2,1,0:T(2,128)S(1)}, u32[]{:S(2)}, u32[]{:S(2)}) %collective-permute-start.4) | collective-permute-done | bytes 110624 | tf_op jit(solution)/shard_map/ppermute | solution.py:42
  65.5 0.9 broadcast_multiply_fusion.2
  66.4 1.5 %fusion.124 = (f32[1,3,2,2,768]{4,0,3,2,1:T(1,128)S(1)}, f32[1,3,2,2,768]{4,0,3,2,1:T(1,128)S(1)}, f32[1,3,2,2,768]{4,0,3,2,1:T(1,128)S(1)}, f32[1,3,2,2,768]{4,...) fusion(f32[2,4,3,1,2,768]{5,1,4,3,2,0:T(4,128)S(1)} %bitcast.66, ...), kind=kLoop, calls=%fused_computation.470 | loop fusion | flops 73728 | bytes 589824 | tf_op jit(solution)/shard_map/stack;squeeze | solution.py:58
  68.2 1.0 fusion.9
  69.3 1.4 %fusion.112 = (f32[1,3,2,2,768]{4,0,3,2,1:T(1,128)S(1)}, f32[1,3,2,2,768]{4,0,3,2,1:T(1,128)S(1)}, f32[1,3,2,2,768]{4,0,3,2,1:T(1,128)S(1)}, f32[1,3,2,2,768]{4,0,3,2,1:T(1,128)S(1)}, f32[1,3,2,2,768]{4,0,3,2,1:T(1,128)S(1)}) fusion(f32[2,4,3,2,1,768]{5,1,4,3,2,0:T(4,128)} %collective-permute-done, f32[2,4,3,2,1,768]{5,1,4,3,2,0:T(4,128)} %copy.474), kind=kLoop, calls=%fused_computation.458 | loop fusion | flops 55296 | bytes 479232 | tf_op jit(solution)/shard_map/stack;squeeze | solution.py:58
  70.7 1.2 %fusion.106 = (f32[1,3,2,2,768]{4,0,3,2,1:T(1,128)S(1)}, f32[1,3,2,2,768]{4,0,3,2,1:T(1,128)S(1)}, f32[1,3,2,2,768]{4,0,3,2,1:T(1,128)S(1)}) fusion(f32[2,4,3,2,1,768]{5,1,4,3,2,0:T(4,128)} %collective-permute-done, f32[2,4,3,2,1,768]{5,1,4,3,2,0:T(4,128)} %copy.474), kind=kLoop, calls=%fused_computation.423 | loop fusion | flops 55296 | bytes 405504 | tf_op jit(solution)/shard_map/mul | solution.py:56
  72.2 1.1 fusion.11
  73.4 1.4 %fusion.116 = (f32[1,3,2,2,768]{4,0,3,2,1:T(1,128)S(1)}, f32[1,3,2,2,768]{4,0,3,2,1:T(1,128)S(1)}, f32[1,3,2,2,768]{4,0,3,2,1:T(1,128)S(1)}, f32[1,3,2,2,768]{4,0,3,2,1:T(1,128)S(1)}, f32[1,3,2,2,768]{4,0,3,2,1:T(1,128)S(1)}) fusion(f32[2,4,3,2,1,768]{5,1,4,3,2,0:T(4,128)} %copy.473, f32[2,4,3,2,1,768]{5,1,4,3,2,0:T(4,128)} %collective-permute-done.2), kind=kLoop, calls=%fused_computation.462 | loop fusion | flops 55296 | bytes 479232 | tf_op jit(solution)/shard_map/stack;squeeze | solution.py:58
  74.8 1.2 %fusion.103 = (f32[1,3,2,2,768]{4,0,3,2,1:T(1,128)S(1)}, f32[1,3,2,2,768]{4,0,3,2,1:T(1,128)S(1)}, f32[1,3,2,2,768]{4,0,3,2,1:T(1,128)S(1)}) fusion(f32[2,4,3,2,1,768]{5,1,4,3,2,0:T(4,128)} %copy.473, f32[2,4,3,2,1,768]{5,1,4,3,2,0:T(4,128)} %collective-permute-done.2), kind=kLoop, calls=%fused_computation.417 | loop fusion | flops 55296 | bytes 405504 | tf_op jit(solution)/shard_map/mul | solution.py:56
  76.3 1.1 fusion.10
  77.5 0.9 broadcast_multiply_fusion
  78.4 1.5 %fusion.132 = (f32[1,3,2,2,768]{4,0,3,2,1:T(1,128)S(1)}, f32[1,3,2,2,768]{4,0,3,2,1:T(1,128)S(1)}, f32[1,3,2,2,768]{4,0,3,2,1:T(1,128)S(1)}, f32[1,3,2,2,768]{4,...) fusion(f32[2,4,3,1,2,768]{5,1,4,3,2,0:T(4,128)} %copy.475, ...), kind=kLoop, calls=%fused_computation.478 | loop fusion | flops 73728 | bytes 589824 | tf_op jit(solution)/shard_map/stack;squeeze | solution.py:58
  80.2 1.0 fusion.8
  82.0 0.7 subtract_reduce_fusion.9
  83.5 0.8 slice_bitcast_fusion.11
  86.4 0.8 fusion.158
  88.7 0.7 slice_bitcast_fusion.9
  90.4 5.3 %collective-permute-start.6 = (f32[2,4,3,2,1,768]{5,1,4,3,2,0:T(4,128)}, f32[2,4,3,2,1,768]{5,1,4,3,2,0:T(4,128)S(1)}, u32[]{:S(2)}, u32[]{:S(2)}) collective-permute-start(f32[2,4,3,2,1,768]{5,1,4,3,2,0:T(4,128)} %get-tuple-element.107), channel_id=1, source_target_pairs={{0,3},{1,0},{2,1},{3,2},{4,7},{5,4},{6,5},{7,6},{8,11},{9,8},{10,9... | collective-permute-start | bytes 442376 | tf_op jit(solution)/shard_map/ppermute | solution.py:42
  95.7 10.9 %collective-permute-start.7 = (f32[2,4,3,1,2,768]{5,1,4,3,2,0:T(4,128)}, f32[2,4,3,1,2,768]{5,1,4,3,2,0:T(4,128)S(1)}, u32[]{:S(2)}, u32[]{:S(2)}) collective-permute-start(f32[2,4,3,1,2,768]{5,1,4,3,2,0:T(4,128)} %get-tuple-element.95), channel_id=1, source_target_pairs={{0,764},{4,0},{8,4},{12,8},{16,12},{20,16},{24,20},{28,24},{32,28}... | collective-permute-start | bytes 442376 | tf_op jit(solution)/shard_map/ppermute | solution.py:42
  106.6 3.0 %add_reduce_fusion.7 = (f32[3,3,2,2,768]{4,3,2,1,0:T(2,128)S(1)}, f32[3,3,2,2,768]{4,3,2,1,0:T(2,128)S(1)}, f32[3,3,2,2,768]{4,3,2,1,0:T(2,128)S(1)}, f32[3,3,2,...) fusion(f32[4,3,2,2,768]{4,0,3,2,1:T(4,128)S(1)} %copy-done.39, ...), kind=kLoop, calls=%fused_computation.136 | loop fusion | flops 3317760 | bytes 2359296 | tf_op jit(solution)/shard_map/reduce_sum | solution.py:94
  112.0 3.0 %add_reduce_fusion.6 = (f32[3,3,2,2,768]{4,3,2,1,0:T(2,128)S(1)}, f32[3,3,2,2,768]{4,3,2,1,0:T(2,128)S(1)}, f32[3,3,2,2,768]{4,3,2,1,0:T(2,128)S(1)}, f32[3,3,2,...) fusion(f32[4,3,2,2,768]{4,0,3,2,1:T(4,128)S(1)} %copy-done.34, ...), kind=kLoop, calls=%fused_computation.134 | loop fusion | flops 3317760 | bytes 2359296 | tf_op jit(solution)/shard_map/reduce_sum | solution.py:94
  119.3 1.3 %pad_maximum_fusion = f32[4,2,3,3,2,2,768]{6,5,4,3,2,1,0:T(2,128)} fusion(f32[1,2,3,3,2,2,768]{6,5,4,3,2,1,0:T(2,128)S(1)} %maximum_bitcast_fusion.3, f32[1,2,3,3,2,2,768]{6,5,4,3,2,1,0:T(2,128)S(1)} %maximum_bitcast_fusion.2, f32[1,2,3,3,2,2,768]{6,5,4,3,2,1,0:T(2,128)S(1)} %maximum_bitcast_fusion.1, f32[1,2,3,3,2,2,768]{6,5,4,3,2,1,0:T(2,128)S(1)} %maximum_bitcast_fusion), kind=kLoop, calls=%fused_computation | loop fusion | flops 663552 | bytes 1769472 | tf_op jit(solution)/shard_map/stack | solution.py:193
  (268 shorter events, 25.4 us)
Async XLA Ops:
  0.6 24.3 %copy-start.1 = (f32[4,2,3,3,2,2,768]{6,5,4,3,2,1,0:T(2,128)S(1)}, f32[4,2,3,3,2,2,768]{6,5,4,3,2,1,0:T(2,128)}, u32[]{:S(2)}) copy-start(f32[4,2,3,3,2,2,768]{6,5,4,3,2,1,0:T(2,128)} %param.4) | copy-start | bytes 2654212
  2.4 31.2 %copy-start = (f32[2,4,3,2,2,768]{5,4,3,2,1,0:T(2,128)S(1)}, f32[2,4,3,2,2,768]{5,4,3,2,1,0:T(2,128)}, u32[]{:S(2)}) copy-start(f32[2,4,3,2,2,768]{5,4,3,2,1,0:T(2,128)} %param.3) | copy-start | bytes 884740
  2.4 63.1 %collective-permute-start.3 = (f32[2,4,3,1,2,768]{5,1,4,3,2,0:T(4,128)}, f32[2,4,3,1,2,768]{5,1,4,3,2,0:T(4,128)}, u32[]{:S(2)}, u32[]{:S(2)}) collective-permute-start(f32[2,4,3,1,2,768]{5,1,4,3,2,0:T(4,128)} %copy.475), channel_id=1, source_target_pairs={{4,0},{8,4},{12,8},{16,12},{20,16},{24,20},{28,24},{32,28},{36,32}... | collective-permute-start | bytes 442376 | tf_op jit(solution)/shard_map/ppermute | solution.py:28
  17.0 52.3 %collective-permute-start = (f32[2,4,3,2,1,768]{5,1,4,3,2,0:T(4,128)}, f32[2,4,3,2,1,768]{5,1,4,3,2,0:T(4,128)}, u32[]{:S(2)}, u32[]{:S(2)}) collective-permute-start(f32[2,4,3,2,1,768]{5,1,4,3,2,0:T(4,128)} %copy.473), channel_id=1, source_target_pairs={{1,0},{2,1},{3,2},{0,3},{5,4},{6,5},{7,6},{4,7},{9,8},{10,9},{11,1... | collective-permute-start | bytes 442376 | tf_op jit(solution)/shard_map/ppermute | solution.py:28
  23.0 50.4 %collective-permute-start.2 = (f32[2,4,3,2,1,768]{5,1,4,3,2,0:T(4,128)}, f32[2,4,3,2,1,768]{5,1,4,3,2,0:T(4,128)}, u32[]{:S(2)}, u32[]{:S(2)}) collective-permute-start(f32[2,4,3,2,1,768]{5,1,4,3,2,0:T(4,128)} %copy.474), channel_id=1, source_target_pairs={{0,1},{1,2},{2,3},{3,0},{4,5},{5,6},{6,7},{7,4},{8,9},{9,10},{10,1... | collective-permute-start | bytes 442376 | tf_op jit(solution)/shard_map/ppermute | solution.py:27
  26.6 30.0 %collective-permute-start.1 = (f32[2,3,3,2,1,768]{5,4,3,2,1,0:T(1,128)}, f32[2,3,3,2,1,768]{5,4,3,2,1,0:T(1,128)}, u32[]{:S(2)}, u32[]{:S(2)}) collective-permute-start(f32[2,3,3,2,1,768]{5,4,3,2,1,0:T(1,128)} %get-tuple-element.232), channel_id=1, source_target_pairs={{0,1},{1,2},{2,3},{3,0},{4,5},{5,6},{6,7},{7,4},{8,9},{9,10},{10,1... | collective-permute-start | bytes 331784 | tf_op jit(solution)/shard_map/ppermute | solution.py:42
  29.5 48.0 %collective-permute-start.5 = (f32[2,4,3,1,2,768]{5,1,4,3,2,0:T(4,128)}, f32[2,4,3,1,2,768]{5,1,4,3,2,0:T(4,128)}, u32[]{:S(2)}, u32[]{:S(2)}) collective-permute-start(f32[2,4,3,1,2,768]{5,1,4,3,2,0:T(4,128)} %copy.476), channel_id=1, source_target_pairs={{0,4},{4,8},{8,12},{12,16},{16,20},{20,24},{24,28},{28,32},{32,36}... | collective-permute-start | bytes 442376 | tf_op jit(solution)/shard_map/ppermute | solution.py:27
  42.1 1.7 %copy-start.2 = (f32[2,4,3,2,2,768]{5,4,3,2,1,0:T(2,128)S(1)}, f32[2,4,3,2,2,768]{5,4,3,2,1,0:T(2,128)}, u32[]{:S(2)}) copy-start(f32[2,4,3,2,2,768]{5,4,3,2,1,0:T(2,128)} %reshape.579) | copy-start | bytes 884740
  45.1 1.6 %copy-start.31 = (f32[1,2,3,3,2,2,768]{6,5,4,3,2,1,0:T(2,128)S(1)}, f32[1,2,3,3,2,2,768]{6,5,4,3,2,1,0:T(2,128)}, u32[]{:S(2)}) copy-start(f32[1,2,3,3,2,2,768]{6,5,4,3,2,1,0:T(2,128)} %get-tuple-element.65) | copy-start | bytes 663556
  50.7 5.1 %copy-start.7 = (f32[4,3,2,2,768]{4,0,3,2,1:T(4,128)}, f32[4,3,2,2,768]{4,0,3,2,1:T(4,128)S(1)}, u32[]{:S(2)}) copy-start(f32[4,3,2,2,768]{4,0,3,2,1:T(4,128)S(1)} %get-tuple-element.188) | copy-start | bytes 442372
  50.7 5.1 %copy-start.9 = (f32[4,3,2,2,768]{4,0,3,2,1:T(4,128)}, f32[4,3,2,2,768]{4,0,3,2,1:T(4,128)S(1)}, u32[]{:S(2)}) copy-start(f32[4,3,2,2,768]{4,0,3,2,1:T(4,128)S(1)} %get-tuple-element.189) | copy-start | bytes 442372
  51.0 1.7 %copy-start.30 = (f32[1,2,3,3,2,2,768]{6,5,4,3,2,1,0:T(2,128)S(1)}, f32[1,2,3,3,2,2,768]{6,5,4,3,2,1,0:T(2,128)}, u32[]{:S(2)}) copy-start(f32[1,2,3,3,2,2,768]{6,5,4,3,2,1,0:T(2,128)} %get-tuple-element.64) | copy-start | bytes 663556
  51.9 1.6 %copy-start.29 = (f32[2,3,3,2,2,768]{5,4,3,2,1,0:T(2,128)S(1)}, f32[2,3,3,2,2,768]{5,4,3,2,1,0:T(2,128)}, u32[]{:S(2)}) copy-start(f32[2,3,3,2,2,768]{5,4,3,2,1,0:T(2,128)} %get-tuple-element.62) | copy-start | bytes 663556
  52.7 1.6 %copy-start.40 = (f32[4,3,2,2,768]{4,3,2,1,0:T(2,128)S(1)}, f32[4,3,2,2,768]{4,3,2,1,0:T(2,128)}, u32[]{:S(2)}) copy-start(f32[4,3,2,2,768]{4,3,2,1,0:T(2,128)} %get-tuple-element.120) | copy-start | bytes 442372
  53.0 2.0 %copy-start.4 = (f32[4,3,2,2,768]{4,0,3,2,1:T(4,128)S(1)}, f32[4,3,2,2,768]{4,0,3,2,1:T(4,128)}, u32[]{:S(2)}) copy-start(f32[4,3,2,2,768]{4,0,3,2,1:T(4,128)} %get-tuple-element.208) | copy-start | bytes 442372
  53.0 2.0 %copy-start.5 = (f32[4,3,2,2,768]{4,0,3,2,1:T(4,128)S(1)}, f32[4,3,2,2,768]{4,0,3,2,1:T(4,128)}, u32[]{:S(2)}) copy-start(f32[4,3,2,2,768]{4,0,3,2,1:T(4,128)} %get-tuple-element.209) | copy-start | bytes 442372
  53.0 2.0 %copy-start.25 = (f32[3,3,2,2,768]{4,3,2,1,0:T(2,128)S(1)}, f32[3,3,2,2,768]{4,3,2,1,0:T(2,128)}, u32[]{:S(2)}) copy-start(f32[3,3,2,2,768]{4,3,2,1,0:T(2,128)} %get-tuple-element.71) | copy-start | bytes 331780
  53.0 2.0 %copy-start.27 = (f32[3,3,2,2,768]{4,3,2,1,0:T(2,128)S(1)}, f32[3,3,2,2,768]{4,3,2,1,0:T(2,128)}, u32[]{:S(2)}) copy-start(f32[3,3,2,2,768]{4,3,2,1,0:T(2,128)} %get-tuple-element.72) | copy-start | bytes 331780
  53.0 2.3 %copy-start.42 = (f32[4,3,2,2,768]{4,0,3,2,1:T(4,128)S(1)}, f32[4,3,2,2,768]{4,0,3,2,1:T(4,128)}, u32[]{:S(2)}) copy-start(f32[4,3,2,2,768]{4,0,3,2,1:T(4,128)} %get-tuple-element.198) | copy-start | bytes 442372
  53.0 2.3 %copy-start.43 = (f32[4,3,2,2,768]{4,0,3,2,1:T(4,128)S(1)}, f32[4,3,2,2,768]{4,0,3,2,1:T(4,128)}, u32[]{:S(2)}) copy-start(f32[4,3,2,2,768]{4,0,3,2,1:T(4,128)} %get-tuple-element.199) | copy-start | bytes 442372
  53.1 2.3 %copy-start.47 = (f32[3,3,2,2,768]{4,3,2,1,0:T(2,128)S(1)}, f32[3,3,2,2,768]{4,3,2,1,0:T(2,128)}, u32[]{:S(2)}) copy-start(f32[3,3,2,2,768]{4,3,2,1,0:T(2,128)} %squeeze.18) | copy-start | bytes 331780
  53.1 2.3 %copy-start.48 = (f32[3,3,2,2,768]{4,3,2,1,0:T(2,128)S(1)}, f32[3,3,2,2,768]{4,3,2,1,0:T(2,128)}, u32[]{:S(2)}) copy-start(f32[3,3,2,2,768]{4,3,2,1,0:T(2,128)} %neg.37) | copy-start | bytes 331780
  53.2 2.6 %copy-start.21 = (f32[3,3,2,2,768]{4,3,2,1,0:T(2,128)S(1)}, f32[3,3,2,2,768]{4,3,2,1,0:T(2,128)}, u32[]{:S(2)}) copy-start(f32[3,3,2,2,768]{4,3,2,1,0:T(2,128)} %get-tuple-element.69) | copy-start | bytes 331780
  53.2 2.6 %copy-start.23 = (f32[3,3,2,2,768]{4,3,2,1,0:T(2,128)S(1)}, f32[3,3,2,2,768]{4,3,2,1,0:T(2,128)}, u32[]{:S(2)}) copy-start(f32[3,3,2,2,768]{4,3,2,1,0:T(2,128)} %get-tuple-element.70) | copy-start | bytes 331780
  53.5 2.7 %copy-start.44 = (f32[4,3,2,2,768]{4,0,3,2,1:T(4,128)S(1)}, f32[4,3,2,2,768]{4,0,3,2,1:T(4,128)}, u32[]{:S(2)}) copy-start(f32[4,3,2,2,768]{4,0,3,2,1:T(4,128)} %get-tuple-element.178) | copy-start | bytes 442372
  53.5 2.7 %copy-start.45 = (f32[4,3,2,2,768]{4,0,3,2,1:T(4,128)S(1)}, f32[4,3,2,2,768]{4,0,3,2,1:T(4,128)}, u32[]{:S(2)}) copy-start(f32[4,3,2,2,768]{4,0,3,2,1:T(4,128)} %get-tuple-element.179) | copy-start | bytes 442372
  54.3 4.4 %copy-start.46 = (f32[2,3,3,2,1,768]{5,4,3,2,1,0:T(1,128)S(1)}, f32[2,3,3,2,1,768]{5,4,3,2,1,0:T(1,128)}, u32[]{:S(2)}) copy-start(f32[2,3,3,2,1,768]{5,4,3,2,1,0:T(1,128)} %get-tuple-element.233) | copy-start | bytes 331780
  56.6 8.8 %collective-permute-start.4 = (f32[2,3,3,1,2,768]{5,4,3,2,1,0:T(2,128)S(1)}, f32[2,3,3,1,2,768]{5,4,3,2,1,0:T(2,128)S(1)}, u32[]{:S(2)}, u32[]{:S(2)}) collective-permute-start(f32[2,3,3,1,2,768]{5,4,3,2,1,0:T(2,128)S(1)} %get-tuple-element.228), channel_id=1, source_target_pairs={{0,4},{4,8},{8,12},{12,16},{16,20},{20,24},{24,28},{28,32},{32,36}... | collective-permute-start | bytes 331784 | tf_op jit(solution)/shard_map/ppermute | solution.py:42
  79.9 2.2 %copy-start.13 = (f32[3,3,2,2,768]{4,3,2,1,0:T(2,128)S(1)}, f32[3,3,2,2,768]{4,3,2,1,0:T(2,128)}, u32[]{:S(2)}) copy-start(f32[3,3,2,2,768]{4,3,2,1,0:T(2,128)} %get-tuple-element.66) | copy-start | bytes 331780
  79.9 2.2 %copy-start.15 = (f32[3,3,2,2,768]{4,3,2,1,0:T(2,128)S(1)}, f32[3,3,2,2,768]{4,3,2,1,0:T(2,128)}, u32[]{:S(2)}) copy-start(f32[3,3,2,2,768]{4,3,2,1,0:T(2,128)} %get-tuple-element.73) | copy-start | bytes 331780
  79.9 2.2 %copy-start.17 = (f32[3,3,2,2,768]{4,3,2,1,0:T(2,128)S(1)}, f32[3,3,2,2,768]{4,3,2,1,0:T(2,128)}, u32[]{:S(2)}) copy-start(f32[3,3,2,2,768]{4,3,2,1,0:T(2,128)} %get-tuple-element.67) | copy-start | bytes 331780
  79.9 2.2 %copy-start.19 = (f32[3,3,2,2,768]{4,3,2,1,0:T(2,128)S(1)}, f32[3,3,2,2,768]{4,3,2,1,0:T(2,128)}, u32[]{:S(2)}) copy-start(f32[3,3,2,2,768]{4,3,2,1,0:T(2,128)} %get-tuple-element.68) | copy-start | bytes 331780
  81.3 1.5 %copy-start.32 = (f32[1,4,3,2,2,768]{5,1,4,3,2,0:T(4,128)S(1)}, f32[1,4,3,2,2,768]{5,1,4,3,2,0:T(4,128)}, u32[]{:S(2)}) copy-start(f32[1,4,3,2,2,768]{5,1,4,3,2,0:T(4,128)} %copy.180) | copy-start | bytes 442372
  81.3 1.5 %copy-start.33 = (f32[1,4,3,2,2,768]{5,1,4,3,2,0:T(4,128)S(1)}, f32[1,4,3,2,2,768]{5,1,4,3,2,0:T(4,128)}, u32[]{:S(2)}) copy-start(f32[1,4,3,2,2,768]{5,1,4,3,2,0:T(4,128)} %copy.179) | copy-start | bytes 442372
  87.8 1.6 %copy-start.49 = (f32[2,4,3,2,2,1,64]{6,5,4,3,2,1,0:T(1,128)S(1)}, f32[2,4,3,2,2,1,64]{6,5,4,3,2,1,0:T(1,128)}, u32[]{:S(2)}) copy-start(f32[2,4,3,2,2,1,64]{6,5,4,3,2,1,0:T(1,128)} %slice.1018) | copy-start | bytes 73732
  89.4 17.2 %copy-start.6 = (f32[4,3,2,2,768]{4,0,3,2,1:T(4,128)S(1)}, f32[4,3,2,2,768]{4,0,3,2,1:T(4,128)}, u32[]{:S(2)}) copy-start(f32[4,3,2,2,768]{4,0,3,2,1:T(4,128)} %get-tuple-element.209) | copy-start | bytes 442372
  89.4 17.2 %copy-start.8 = (f32[4,3,2,2,768]{4,0,3,2,1:T(4,128)S(1)}, f32[4,3,2,2,768]{4,0,3,2,1:T(4,128)}, u32[]{:S(2)}) copy-start(f32[4,3,2,2,768]{4,0,3,2,1:T(4,128)} %copy-done.7) | copy-start | bytes 442372
  89.4 17.2 %copy-start.10 = (f32[4,3,2,2,768]{4,0,3,2,1:T(4,128)S(1)}, f32[4,3,2,2,768]{4,0,3,2,1:T(4,128)}, u32[]{:S(2)}) copy-start(f32[4,3,2,2,768]{4,0,3,2,1:T(4,128)} %copy-done.9) | copy-start | bytes 442372
  89.4 17.2 %copy-start.38 = (f32[4,3,2,2,768]{4,0,3,2,1:T(4,128)S(1)}, f32[4,3,2,2,768]{4,0,3,2,1:T(4,128)}, u32[]{:S(2)}) copy-start(f32[4,3,2,2,768]{4,0,3,2,1:T(4,128)} %get-tuple-element.132) | copy-start | bytes 442372
  89.4 17.2 %copy-start.39 = (f32[4,3,2,2,768]{4,0,3,2,1:T(4,128)S(1)}, f32[4,3,2,2,768]{4,0,3,2,1:T(4,128)}, u32[]{:S(2)}) copy-start(f32[4,3,2,2,768]{4,0,3,2,1:T(4,128)} %get-tuple-element.133) | copy-start | bytes 442372
  90.4 19.8 %collective-permute-start.6 = (f32[2,4,3,2,1,768]{5,1,4,3,2,0:T(4,128)}, f32[2,4,3,2,1,768]{5,1,4,3,2,0:T(4,128)S(1)}, u32[]{:S(2)}, u32[]{:S(2)}) collective-permute-start(f32[2,4,3,2,1,768]{5,1,4,3,2,0:T(4,128)} %get-tuple-element.107), channel_id=1, source_target_pairs={{0,3},{1,0},{2,1},{3,2},{4,7},{5,4},{6,5},{7,6},{8,11},{9,8},{10,9... | collective-permute-start | bytes 442376 | tf_op jit(solution)/shard_map/ppermute | solution.py:42
  95.7 15.3 %collective-permute-start.7 = (f32[2,4,3,1,2,768]{5,1,4,3,2,0:T(4,128)}, f32[2,4,3,1,2,768]{5,1,4,3,2,0:T(4,128)S(1)}, u32[]{:S(2)}, u32[]{:S(2)}) collective-permute-start(f32[2,4,3,1,2,768]{5,1,4,3,2,0:T(4,128)} %get-tuple-element.95), channel_id=1, source_target_pairs={{0,764},{4,0},{8,4},{12,8},{16,12},{20,16},{24,20},{28,24},{32,28}... | collective-permute-start | bytes 442376 | tf_op jit(solution)/shard_map/ppermute | solution.py:42
  111.7 3.6 %copy-start.26 = (f32[3,3,2,2,768]{4,3,2,1,0:T(2,128)S(1)}, f32[3,3,2,2,768]{4,3,2,1,0:T(2,128)}, u32[]{:S(2)}) copy-start(f32[3,3,2,2,768]{4,3,2,1,0:T(2,128)} %get-tuple-element.71) | copy-start | bytes 331780
  111.7 3.6 %copy-start.28 = (f32[3,3,2,2,768]{4,3,2,1,0:T(2,128)S(1)}, f32[3,3,2,2,768]{4,3,2,1,0:T(2,128)}, u32[]{:S(2)}) copy-start(f32[3,3,2,2,768]{4,3,2,1,0:T(2,128)} %get-tuple-element.72) | copy-start | bytes 331780
  115.4 1.6 %copy-start.18 = (f32[3,3,2,2,768]{4,3,2,1,0:T(2,128)S(1)}, f32[3,3,2,2,768]{4,3,2,1,0:T(2,128)}, u32[]{:S(2)}) copy-start(f32[3,3,2,2,768]{4,3,2,1,0:T(2,128)} %get-tuple-element.67) | copy-start | bytes 331780
  115.4 1.6 %copy-start.20 = (f32[3,3,2,2,768]{4,3,2,1,0:T(2,128)S(1)}, f32[3,3,2,2,768]{4,3,2,1,0:T(2,128)}, u32[]{:S(2)}) copy-start(f32[3,3,2,2,768]{4,3,2,1,0:T(2,128)} %get-tuple-element.68) | copy-start | bytes 331780
  116.2 1.6 %copy-start.14 = (f32[3,3,2,2,768]{4,3,2,1,0:T(2,128)S(1)}, f32[3,3,2,2,768]{4,3,2,1,0:T(2,128)}, u32[]{:S(2)}) copy-start(f32[3,3,2,2,768]{4,3,2,1,0:T(2,128)} %get-tuple-element.66) | copy-start | bytes 331780
  116.2 1.6 %copy-start.16 = (f32[3,3,2,2,768]{4,3,2,1,0:T(2,128)S(1)}, f32[3,3,2,2,768]{4,3,2,1,0:T(2,128)}, u32[]{:S(2)}) copy-start(f32[3,3,2,2,768]{4,3,2,1,0:T(2,128)} %get-tuple-element.73) | copy-start | bytes 331780
  (10 other events, 11.1 us)
where the time goes:
time: 122 us; the launch traced here: 121 us
  starting transfers between devices  44.3 us (36%)
  other arithmetic  39.4 us (32%)
  local copies, waits for them, and re-layouts  28.8 us (24%)
  waiting for transfers between devices  5.64 us (5%)
  between operations  2.49 us (2%)
    ppermute x4, starting transfers between devices, passed_along(): return lax.ppermute(value, axis, pairs)  20.4 us
    ppermute x2, starting transfers between devices, padded(): lax.ppermute(leading, axis, [(b, a) for a, b in up])  17.8 us
    another operation x28, other arithmetic, apply_gamma(): return jnp.stack([jnp.stack(parts_re), jnp.stack(parts_im)])  9.66 us
    unnamed x153, local copies, waits for them, and re-layouts  6.56 us
    reduce_sum x2, other arithmetic, spin_outer(): out_re = jnp.sum(left_re * right_re + left_im * right_im, axis=0)  6.07 us
    ppermute x2, starting transfers between devices, padded(): lax.ppermute(last, axis, up)  6.06 us
    ppermute x4, waiting for transfers between devices, passed_along(): return lax.ppermute(value, axis, pairs)  5.62 us
    add x12, other arithmetic, project(): return field + sign * apply_gamma(hop_dir, field)  5.23 us
  transfers between devices with their start and end apart: 8, of which 1 were waited for; matrix products, arithmetic and copies ran while one was open for 36% of the time, Pallas kernels for 0%

commit v1 on v0

v1 whole, which is shorter than its diff:
```python
import jax
import jax.numpy as jnp
from jax import lax
from jax.experimental import pallas as pl
from jax.experimental.pallas import tpu as pltpu
from jax.sharding import PartitionSpec as P


F32 = jnp.float32
LANES = 128
DIAG = 3.75
PAIRED = ('ta', 'gz')
gamma_table = (
    ((3, 0, -1), (2, 0, -1), (1, 0, 1), (0, 0, 1)),
    ((3, -1, 0), (2, 1, 0), (1, 1, 0), (0, -1, 0)),
    ((2, 0, -1), (3, 0, 1), (0, 0, 1), (1, 0, -1)),
    ((2, 1, 0), (3, 1, 0), (0, 1, 0), (1, 1, 0)),
)


def add(x, y, sign):
    return x + y if sign > 0 else x - y


def half(psi, mu, sign):
    out = []
    for s in range(2):
        src, pr, pi = gamma_table[mu][s]
        row = []
        for a in range(3):
            re, im = psi[s][a]
            sre, sim = psi[src][a]
            if pi == 0:
                row.append((add(re, sre, sign * pr), add(im, sim, sign * pr)))
            else:
                row.append((add(re, sim, -sign * pi), add(im, sre, sign * pi)))
        out.append(row)
    return out


def phase(mu, r, h):
    src, pr, pi = gamma_table[mu][r]
    if pi == 0:
        return [((pr, re), (pr, im)) for re, im in h[src]]
    return [((-pi, im), (pi, re)) for re, im in h[src]]


def cmul(u, h):
    out = []
    for s in range(2):
        row = []
        for a in range(3):
            re = im = None
            for b in range(3):
                ur, ui = u[a][b]
                hr, hi = h[s][b]
                r = ur * hr - ui * hi
                i = ur * hi + ui * hr
                re = r if re is None else re + r
                im = i if im is None else im + i
            row.append((re, im))
        out.append(row)
    return out


def cmul_dag(u, h):
    out = []
    for s in range(2):
        row = []
        for a in range(3):
            re = im = None
            for b in range(3):
                ur, ui = u[b][a]
                hr, hi = h[s][b]
                r = ur * hr + ui * hi
                i = ur * hi - ui * hr
                re = r if re is None else re + r
                im = i if im is None else im + i
            row.append((re, im))
        out.append(row)
    return out


def hmap(f, h):
    return [[(f(re), f(im)) for re, im in row] for row in h]


def hmap2(f, g, h):
    return [[(f(x[0], y[0]), f(x[1], y[1])) for x, y in zip(p, q)] for p, q in zip(g, h)]


def accumulate(acc, mu, h, sign):
    for s in range(2):
        for a in range(3):
            acc[s][a] = (acc[s][a][0] + h[s][a][0], acc[s][a][1] + h[s][a][1])
    signed = h if isinstance(sign, int) else hmap(lambda v: v * sign, h)
    flip = sign if isinstance(sign, int) else 1
    for r in range(2, 4):
        for a, ((gr, vr), (gi, vi)) in enumerate(phase(mu, r, signed)):
            acc[r][a] = (add(acc[r][a][0], vr, flip * gr), add(acc[r][a][1], vi, flip * gi))


def rows_of(k):
    return slice(8 * k, 8 * k + 8)


def get_spinor(ref, index):
    return [[(ref[3 * s + a, index, :], ref[12 + 3 * s + a, index, :]) for a in range(3)] for s in range(4)]


def get_link(ref, d, index):
    return [[(ref[18 * d + 3 * a + b, index, :], ref[18 * d + 9 + 3 * a + b, index, :]) for b in range(3)] for a in range(3)]


def get_half(ref, index):
    return [[(ref[3 * s + a, index, :], ref[6 + 3 * s + a, index, :]) for a in range(3)] for s in range(2)]


def put_half(ref, index, h):
    for s in range(2):
        for a in range(3):
            ref[3 * s + a, index, :] = h[s][a][0]
            ref[6 + 3 * s + a, index, :] = h[s][a][1]


def put_spinor(ref, index, psi):
    for s in range(4):
        for a in range(3):
            ref[3 * s + a, index, :] = psi[s][a][0]
            ref[12 + 3 * s + a, index, :] = psi[s][a][1]


def iotas():
    lane = lax.broadcasted_iota(jnp.int32, (8, LANES), 1)
    row = lax.broadcasted_iota(jnp.int32, (8, LANES), 0)
    return lane, row


def shift_x(v, step):
    lane = lax.broadcasted_iota(jnp.int32, (8, LANES), 1) % 64
    if step > 0:
        return jnp.where(lane == 63, pltpu.roll(v, 63, 1), pltpu.roll(v, LANES - 1, 1))
    return jnp.where(lane == 0, pltpu.roll(v, 65, 1), pltpu.roll(v, 1, 1))


def shift_y(here, other, step):
    lane, row = iotas()
    low = row < 4
    mixed = jnp.where(low, other, here) if step > 0 else jnp.where(low, here, other)
    keep = lane >= 64 if step > 0 else lane < 64
    return pltpu.roll(jnp.where(keep, here, pltpu.roll(mixed, 4, 0)), 64, 1)


def shift_rows(v, count, step):
    return pltpu.roll(v, 8 - count if step > 0 else count, 0)


def is_even(axis):
    return lax.axis_index(axis) % 2 == 0


def outgoing(axis, up, dn):
    if axis not in PAIRED:
        return up, dn
    even = is_even(axis)
    return jnp.where(even, up, dn), jnp.where(even, dn, up)


def sent_up(axis, first, second, index):
    if axis not in PAIRED:
        return first[index]
    return jnp.where(is_even(axis), first[index], second[index])


def from_below(axis, first, second, index):
    if axis not in PAIRED:
        return first[index]
    return jnp.where(is_even(axis), second[index], first[index])


def from_above(axis, first, second, index):
    if axis not in PAIRED:
        return second[index]
    return jnp.where(is_even(axis), first[index], second[index])


def plane_copies(src, dst, sems, out=False):
    copies = []
    tiles = dst.shape[-3] // 2
    lead = (slice(None),) * (len(dst.shape) - 3)
    for t in range(2):
        for j in range(tiles):
            wide = src.at[lead + (t, slice(None), pl.ds(LANES * j, LANES))]
            packed = dst.at[lead + (2 * j + t,)]
            pair = (packed, wide) if out else (wide, packed)
            copies.append(pltpu.make_async_copy(*pair, sems.at[2 * j + t]))
    return copies


def flat(ref):
    shape = ref.shape
    lead = 1
    for n in shape[:-3]:
        lead *= n
    return ref.reshape(lead, 2 * shape[-3], LANES)


def put_face(ref, part, h):
    for s in range(2):
        for a in range(3):
            ref[pl.ds(12 * (3 * s + a) + 6 * part, 6), :] = h[s][a][0]
            ref[pl.ds(12 * (6 + 3 * s + a) + 6 * part, 6), :] = h[s][a][1]


def face_rows(t, z):
    return pl.ds(2 * t + z, 6, stride=4)


def halo_row(c, part):
    return (pl.ds(12 * c + 6 * part, 6), slice(None))


def faces_kernel(spinor, links, s_out, l_out, t_a, t_b, z_a, z_b, sem_s, sem_l):
    copies = plane_copies(spinor, s_out, sem_s) + plane_copies(links.at[pl.ds(2, 2)], l_out, sem_l)
    for c in copies:
        c.start()
    place = lax.axis_index("ta")
    up_sign = jnp.where(place == lax.axis_size("ta") - 1, -1.0, 1.0).astype(F32)
    dn_sign = jnp.where(place == 0, -1.0, 1.0).astype(F32)
    for c in copies:
        c.wait()
    s_ref, l_ref = flat(s_out), flat(l_out)
    for part in range(2):
        for axis, mu, d, first, second, low, high in (
            ("gz", 2, 0, z_a, z_b, face_rows(part, 0), face_rows(part, 1)),
            ("ta", 3, 1, t_a, t_b, face_rows(0, part), face_rows(1, part)),
        ):
            dn = half(get_spinor(s_ref, low), mu, -1)
            up = cmul_dag(get_link(l_ref, d, high), half(get_spinor(s_ref, high), mu, 1))
            if axis == "ta":
                dn = hmap(lambda v: v * dn_sign, dn)
                up = hmap(lambda v: v * up_sign, up)
            put_face(first, part, hmap2(lambda x, y: outgoing(axis, x, y)[0], up, dn))
            put_face(second, part, hmap2(lambda x, y: outgoing(axis, x, y)[1], up, dn))


def local_kernel(s_in, l_in, links, clover, p_out, l_out, c_ref, chi, sem_l, sem_c):
    copies_l = plane_copies(links.at[pl.ds(0, 2)], l_out, sem_l)
    copies_c = plane_copies(clover, c_ref, sem_c)
    for c in copies_l + copies_c:
        c.start()
    s_ref, l23, l01, cl = flat(s_in), flat(l_in), flat(l_out), flat(c_ref)
    _, row = iotas()
    low_z = row % 2 == 0
    low_t = (row // 2) % 2 == 0
    sign_z = jnp.where(low_z, -1.0, 1.0)
    sign_t = jnp.where(low_t, -1.0, 1.0)
    zero = jnp.zeros((8, LANES), F32)
    for k in range(3):
        psi = get_spinor(s_ref, rows_of(k))
        acc = [[(zero, zero) for _ in range(3)] for _ in range(4)]
        for mu, d, n, low, sign in ((2, 0, 1, low_z, sign_z), (3, 1, 2, low_t, sign_t)):
            u = get_link(l23, d, rows_of(k))
            ahead = cmul(u, hmap(lambda v: shift_rows(v, n, 1), half(psi, mu, -1)))
            behind = hmap(lambda v: shift_rows(v, n, -1), cmul_dag(u, half(psi, mu, 1)))
            accumulate(acc, mu, hmap2(lambda x, y: jnp.where(low, x, y), ahead, behind), sign)
        put_spinor(p_out, rows_of(k), acc)
    for c in copies_l:
        c.wait()
    for k in range(3):
        put_half(chi, rows_of(k), cmul_dag(get_link(l01, 1, rows_of(k)), half(get_spinor(s_ref, rows_of(k)), 1, 1)))
    for k in range(3):
        psi = get_spinor(s_ref, rows_of(k))
        acc = get_spinor(p_out, rows_of(k))
        u = get_link(l01, 0, rows_of(k))
        accumulate(acc, 0, cmul(u, hmap(lambda v: shift_x(v, 1), half(psi, 0, -1))), -1)
        accumulate(acc, 0, hmap(lambda v: shift_x(v, -1), cmul_dag(u, half(psi, 0, 1))), 1)
        u = get_link(l01, 1, rows_of(k))
        nxt = half(get_spinor(s_ref, rows_of((k + 1) % 3)), 1, -1)
        ahead = hmap2(lambda x, y: shift_y(x, y, 1), half(psi, 1, -1), nxt)
        accumulate(acc, 1, cmul(u, ahead), -1)
        behind = hmap2(lambda x, y: shift_y(x, y, -1), get_half(chi, rows_of(k)), get_half(chi, rows_of((k + 2) % 3)))
        accumulate(acc, 1, behind, 1)
        put_spinor(p_out, rows_of(k), acc)
    for c in copies_c:
        c.wait()
    for k in range(3):
        for chirality in range(2):
            field = [[(s_ref[6 * chirality + i, rows_of(k), :], s_ref[12 + 6 * chirality + i, rows_of(k), :])] for i in range(6)]
            for i in range(6):
                re = DIAG * field[i][0][0] - 0.5 * p_out[6 * chirality + i, rows_of(k), :]
                im = DIAG * field[i][0][1] - 0.5 * p_out[12 + 6 * chirality + i, rows_of(k), :]
                for j in range(6):
                    cr = cl[36 * chirality + 6 * i + j, rows_of(k), :]
                    ci = cl[72 + 36 * chirality + 6 * i + j, rows_of(k), :]
                    fr, fi = field[j][0]
                    re = re + (cr * fr - ci * fi)
                    im = im + (cr * fi + ci * fr)
                p_out[6 * chirality + i, rows_of(k), :] = re
                p_out[12 + 6 * chirality + i, rows_of(k), :] = im


def low_rows(mu):
    row = lax.broadcasted_iota(jnp.int32, (8, LANES), 0)
    return (row if mu == 2 else row // 2) % 2 == 0


def spread(dst, mu, level, value):
    for c in range(12):
        for part in range(2):
            first = 2 * part + level if mu == 2 else 2 * level + part
            dst[c, pl.ds(first, 6, stride=4), :] = value(c, part)


def add_halo(acc, mu, u, h):
    low = low_rows(mu)
    term = hmap2(lambda x, y: -0.5 * jnp.where(low, x, y), h, cmul(u, h))
    accumulate(acc, mu, term, jnp.where(low, 1.0, -1.0))


def halo_kernel(mu, p_in, l_in, first, second, a_out, face, halo):
    axis = "gz" if mu == 2 else "ta"
    l23 = flat(l_in)
    a_ref = flat(a_out) if len(a_out.shape) > 3 else a_out
    spread(halo, mu, 0, lambda c, part: from_below(axis, first, second, halo_row(c, part)))
    spread(halo, mu, 1, lambda c, part: from_above(axis, first, second, halo_row(c, part)))
    for k in range(3):
        acc = get_spinor(p_in, rows_of(k))
        add_halo(acc, mu, get_link(l23, mu - 2, rows_of(k)), get_half(halo, rows_of(k)))
        put_spinor(a_ref, rows_of(k), acc)
    dn_sign = jnp.where(lax.axis_index("ta") == 0, -1.0, 1.0).astype(F32)
    for part in range(2):
        if mu == 3:
            put_face(face, part, half(get_spinor(a_ref, face_rows(part, 0)), 2, 1))
        else:
            out = half(get_spinor(a_ref, face_rows(0, part)), 3, 1)
            put_face(face, part, hmap(lambda v: v * dn_sign, out))


def mid_kernel(*refs):
    halo_kernel(3, *refs)


def finish_kernel(*refs):
    halo_kernel(2, *refs)


def outer(left, right, total=None):
    out = []
    for a in range(3):
        row = []
        for b in range(3):
            re, im = (None, None) if total is None else total[a][b]
            for s in range(2):
                lr, li = left[s][a]
                rr, ri = right[s][b]
                r = lr * rr + li * ri
                i = li * rr - lr * ri
                re = r if re is None else re + r
                im = i if im is None else im + i
            row.append((re, im))
        out.append(row)
    return out


def put_force(ref, d, index, u, m):
    w = []
    for a in range(3):
        row = []
        for b in range(3):
            re = im = None
            for c in range(3):
                ur, ui = u[a][c]
                mr, mi = m[c][b]
                i = ur * mi + ui * mr
                im = i if im is None else im + i
                if a != b:
                    r = ur * mr - ui * mi
                    re = r if re is None else re + r
            row.append((re, im))
        w.append(row)
    third = (w[0][0][1] + w[1][1][1] + w[2][2][1]) * (1.0 / 3.0)
    for a in range(3):
        ref[18 * d + 4 * a, index, :] = jnp.zeros((8, LANES), F32)
        ref[18 * d + 9 + 4 * a, index, :] = w[a][a][1] - third
        for b in range(a + 1, 3):
            re = 0.5 * (w[a][b][0] - w[b][a][0])
            im = 0.5 * (w[a][b][1] + w[b][a][1])
            ref[18 * d + 3 * a + b, index, :] = re
            ref[18 * d + 3 * b + a, index, :] = -re
            ref[18 * d + 9 + 3 * a + b, index, :] = im
            ref[18 * d + 9 + 3 * b + a, index, :] = im


def get_matrix(ref, d, index):
    return get_link(ref, d, index)


def put_matrix(ref, d, index, m):
    for a in range(3):
        for b in range(3):
            ref[18 * d + 3 * a + b, index, :] = m[a][b][0]
            ref[18 * d + 9 + 3 * a + b, index, :] = m[a][b][1]


def plane_kernel(s_in, a_in, l_in, t_a, t_b, z_a, z_b, applied, force, m_out, f_ref, halo, sem_a, sem_f):
    copies = plane_copies(applied, a_in, sem_a, out=True)
    for c in copies:
        c.start()
    s_ref, a_ref, l01, f = flat(s_in), flat(a_in), flat(l_in), flat(f_ref)
    for k in range(3):
        psi = get_spinor(s_ref, rows_of(k))
        app = get_spinor(a_ref, rows_of(k))
        m = outer(hmap(lambda v: shift_x(v, 1), half(psi, 0, -1)), half(app, 0, -1))
        m = outer(hmap(lambda v: shift_x(v, 1), half(app, 0, 1)), half(psi, 0, 1), m)
        put_force(f, 0, rows_of(k), get_link(l01, 0, rows_of(k)), m)
        psi_n = half(get_spinor(s_ref, rows_of((k + 1) % 3)), 1, -1)
        app_n = half(get_spinor(a_ref, rows_of((k + 1) % 3)), 1, 1)
        m = outer(hmap2(lambda x, y: shift_y(x, y, 1), half(psi, 1, -1), psi_n), half(app, 1, -1))
        m = outer(hmap2(lambda x, y: shift_y(x, y, 1), half(app, 1, 1), app_n), half(psi, 1, 1), m)
        put_force(f, 1, rows_of(k), get_link(l01, 1, rows_of(k)), m)
    out = plane_copies(force.at[pl.ds(0, 2)], f_ref, sem_f, out=True)
    for c in out:
        c.start()
    for mu, axis, first, second in ((2, "gz", z_a, z_b), (3, "ta", t_a, t_b)):
        low = low_rows(mu)
        spread(halo, mu, 1, lambda c, part: from_above(axis, first, second, halo_row(c, part)))
        for k in range(3):
            psi = get_spinor(s_ref, rows_of(k))
            app = get_spinor(a_ref, rows_of(k))
            near = hmap(lambda v: shift_rows(v, mu - 1, 1), half(psi, mu, -1))
            ahead = hmap2(lambda x, y: jnp.where(low, x, y), near, get_half(halo, rows_of(k)))
            m = outer(ahead, half(app, mu, -1))
            ahead = hmap(lambda v: jnp.where(low, shift_rows(v, mu - 1, 1), 0.0), half(app, mu, 1))
            m = outer(ahead, half(psi, mu, 1), m)
            put_matrix(m_out, mu - 2, rows_of(k), m)
    for c in copies + out:
        c.wait()


def edge_kernel(s_in, l_in, m_in, a_t, a_z, z_a, z_b, force_in, force, f_ref, halo, sem_f):
    s_ref, l23, f = flat(s_in), flat(l_in), flat(f_ref)
    out = []
    for d, mu in ((1, 3), (0, 2)):
        for c in range(12):
            for k in range(3):
                halo[c, rows_of(k), :] = jnp.zeros((8, LANES), F32)
        if mu == 3:
            spread(halo, mu, 1, lambda c, part: a_t[halo_row(c, part)])
        else:
            spread(halo, mu, 1, lambda c, part: a_z[halo_row(c, part)] - sent_up("gz", z_a, z_b, halo_row(c, part)))
        for k in range(3):
            psi = half(get_spinor(s_ref, rows_of(k)), mu, 1)
            m = outer(get_half(halo, rows_of(k)), psi, get_matrix(m_in, d, rows_of(k)))
            put_force(f, d, rows_of(k), get_link(l23, d, rows_of(k)), m)
        copies = plane_copies(force.at[pl.ds(mu, 1)], f_ref.at[pl.ds(d, 1)], sem_f.at[d], out=True)
        for c in copies:
            c.start()
        out += copies
    for c in out:
        c.wait()


HBM = pl.BlockSpec(memory_space=pltpu.HBM)
VMEM = pl.BlockSpec(memory_space=pltpu.VMEM)
LIMIT = 12 * 1024 * 1024


def call(kernel, ins, outs, scratch, args, aliases=None):
    return pl.pallas_call(
        kernel,
        out_shape=tuple(jax.ShapeDtypeStruct(shape, F32) for shape, _ in outs),
        in_specs=list(ins),
        out_specs=tuple(spec for _, spec in outs),
        scratch_shapes=list(scratch),
        compiler_params=pltpu.CompilerParams(vmem_limit_bytes=LIMIT),
        input_output_aliases=aliases or {},
    )(*args)


def moved(value, axis, step):
    count = lax.axis_size(axis)
    return lax.ppermute(value, axis, [(i, (i + step) % count) for i in range(count)])


def swapped(value, axis, start):
    count = lax.axis_size(axis)
    pairs = [(i % count, (i + 1) % count) for i in range(start, count + start, 2)]
    return lax.ppermute(value, axis, pairs + [(b, a) for a, b in pairs])


def exchanged(axis, first, second):
    if axis in PAIRED:
        return swapped(first, axis, 0), swapped(second, axis, 1)
    return moved(first, axis, 1), moved(second, axis, -1)


def steps(spinor, links, clover):
    tiles = spinor.shape[-1] // LANES
    packed = (2 * tiles, 2, LANES)
    s_shape = (2, 4, 3) + packed
    l_shape = (2, 2, 3, 3) + packed
    c_shape = (2, 2, 6, 6) + packed
    rows = (4 * tiles, LANES)
    face = ((24 * tiles, LANES), VMEM)
    halo = pltpu.VMEM((12,) + rows, F32)
    dma = pltpu.SemaphoreType.DMA((2 * tiles,))
    spinor, links, clover = (pltpu.with_memory_space_constraint(x, pltpu.HBM) for x in (spinor, links, clover))
    s, l23, t_a, t_b, z_a, z_b = call(
        faces_kernel, (HBM, HBM), ((s_shape, VMEM), (l_shape, VMEM), face, face, face, face),
        (dma, dma), (spinor, links),
    )
    z_sent = (z_a, z_b)
    z_a, z_b = exchanged("gz", z_a, z_b)
    t_a, t_b = exchanged("ta", t_a, t_b)
    p, l01 = call(
        local_kernel, (VMEM, VMEM, HBM, HBM), (((24,) + rows, VMEM), (l_shape, VMEM)),
        (pltpu.VMEM(c_shape, F32), halo, dma, dma), (s, l23, links, clover),
    )
    p, a_z = call(mid_kernel, (VMEM,) * 4, (((24,) + rows, VMEM), face), (halo,), (p, l23, t_a, t_b))
    a_z = moved(a_z, "gz", -1)
    a, a_t = call(finish_kernel, (VMEM,) * 4, ((s_shape, VMEM), face), (halo,), (p, l23, z_a, z_b))
    a_t = moved(a_t, "ta", -1)
    applied, force, m = call(
        plane_kernel, (VMEM,) * 7, ((spinor.shape, HBM), (links.shape, HBM), ((36,) + rows, VMEM)),
        (pltpu.VMEM(l_shape, F32), halo, dma, dma), (s, a, l01, t_a, t_b, z_a, z_b),
    )
    (force,) = call(
        edge_kernel, (VMEM,) * 7 + (HBM,), ((links.shape, HBM),),
        (pltpu.VMEM(l_shape, F32), halo, pltpu.SemaphoreType.DMA((2, 2 * tiles))),
        (s, l23, m, a_t, a_z) + z_sent + (force,), {7: 0},
    )
    return applied, force


def solution(mesh):
    spin = P(None, None, None, "ta", "gz", None)
    link = P(None, None, None, None, "ta", "gz", None)
    return jax.shard_map(steps, mesh=mesh, in_specs=(spin, link, link), out_specs=(spin, link), check_vma=False)
```

time: 122 us -> 47.8 us (0.39)
  other arithmetic: 39.4 us -> 0 us
  local copies, waits for them, and re-layouts: 28.8 us -> 0 us
  Pallas kernels: 0 us -> 7.19 us
  starting transfers between devices: 44.3 us -> 37.6 us
  waiting for transfers between devices: 5.64 us -> 1.88 us
  between operations: 2.49 us -> 0.74 us
    reduce_sum x14 -> x0, other arithmetic: 12.4 us -> none  [the longest x2 6.07 us: spin_outer(): out_re = jnp.sum(left_re * right_re + left_im * right_im, axis=0)]
    another operation x38 -> x0, other arithmetic: 11.8 us -> none  [the longest x28 9.66 us: apply_gamma(): return jnp.stack([jnp.stack(parts_re), jnp.stack(parts_im)])]
    pallas_call x0 -> x6, Pallas kernels: none -> 7.19 us  [call(): pl.pallas_call(kernel, out_shape=tuple((jax.ShapeDtypeStruct(shape, F32)...]
    mul x21 -> x0, local copies, waits for them, and re-layouts: 7.17 us -> none  [the longest x8 3.84 us: spin_outer(): out_re = jnp.sum(left_re * right_re + left_im * right_im, axis=0)]
    slice x15 -> x0, local copies, waits for them, and re-layouts: 6.88 us -> none  [the longest x2 2.45 us: slab(): return lax.slice_in_dim(field, start, stop, axis=dimension)]
    ppermute x8 -> x6, starting transfers between devices: 44.3 us -> 37.6 us  [the longest x4 24.1 us: swapped(): return lax.ppermute(value, axis, pairs + [(b, a) for a, b in pairs])]
    unnamed x153 -> x0, local copies, waits for them, and re-layouts: 6.56 us -> none
    add x16 -> x0, other arithmetic: 5.98 us -> none  [the longest x12 5.23 us: project(): return field + sign * apply_gamma(hop_dir, field)]
  transfers between devices with their start and end apart: 8 -> 6, of which waited for: 1 -> 2; matrix products, arithmetic and copies ran while one was open for 36% -> 0% of each run, Pallas kernels for 0% -> 9%
where the time goes in v1:
time: 47.8 us; the launch traced here: 47.4 us
  starting transfers between devices  37.6 us (79%)
  Pallas kernels  7.19 us (15%)
  waiting for transfers between devices  1.88 us (4%)
  between operations  0.74 us (2%)
    ppermute x4, starting transfers between devices, swapped(): return lax.ppermute(value, axis, pairs + [(b, a) for a, b in pairs])  24.1 us
    ppermute x2, starting transfers between devices, moved(): lax.ppermute(value, axis, [(i, (i + step) % count) for i in range(count)])  13.6 us
    pallas_call x6, Pallas kernels, call(): pl.pallas_call(kernel, out_shape=tuple((jax.ShapeDtypeStruct(shape, F32)...  7.19 us
    ppermute x4, waiting for transfers between devices, swapped(): return lax.ppermute(value, axis, pairs + [(b, a) for a, b in pairs])  1.74 us
  transfers between devices with their start and end apart: 6, of which 2 were waited for; matrix products, arithmetic and copies ran while one was open for 0% of the time, Pallas kernels for 9%

profile of v1, /device:TPU:1, one launch (start us, length us, event | category | flops | bytes accessed | tf_op | source)
XLA Modules:
  0.0 47.4 jit_solution(17361732877364692055)
XLA Ops:
  0.6 1.5 %shard_map.50 = (f32[2,4,3,12,2,128]{5,4,3,2,1,0:T(2,128)S(1)}, f32[2,2,3,3,12,2,128]{6,5,4,3,2,1,0:T(2,128)S(1)}, f32[144,128]{1,0:T(8,128)S(1)}, f32[144,128]{...) custom-call(f32[2,4,3,2,2,768]{5,4,3,2,1,0:T(2,128)} %spinor.1, f32[4,2,3,3,2,2,768]{6,5,4,3,2,1,0:T(2,128)} %links.3), custom_call_target="tpu_custom_call" | custom-call | tf_op jit(solution)/shard_map/pallas_call | solution.py:470
  2.1 12.4 %collective-permute-start = (f32[144,128]{1,0:T(8,128)S(1)}, f32[144,128]{1,0:T(8,128)S(1)}, u32[]{:S(2)}, u32[]{:S(2)}) collective-permute-start(f32[144,128]{1,0:T(8,128)S(1)} %get-tuple-element.20), channel_id=1, source_target_pairs={{0,4},{8,12},{16,20},{24,28},{32,36},{40,44},{48,52},{56,60},{64,6... | collective-permute-start | bytes 221192 | tf_op jit(solution)/shard_map/ppermute | solution.py:489
  14.5 1.9 %collective-permute-start.1 = (f32[144,128]{1,0:T(8,128)S(1)}, f32[144,128]{1,0:T(8,128)S(1)}, u32[]{:S(2)}, u32[]{:S(2)}) collective-permute-start(f32[144,128]{1,0:T(8,128)S(1)} %get-tuple-element.21), channel_id=1, source_target_pairs={{4,8},{12,16},{20,24},{28,32},{36,40},{44,48},{52,56},{60,64},{68,... | collective-permute-start | bytes 221192 | tf_op jit(solution)/shard_map/ppermute | solution.py:489
  16.4 1.9 %collective-permute-start.2 = (f32[144,128]{1,0:T(8,128)S(1)}, f32[144,128]{1,0:T(8,128)S(1)}, u32[]{:S(2)}, u32[]{:S(2)}) collective-permute-start(f32[144,128]{1,0:T(8,128)S(1)} %get-tuple-element.23.z_a), channel_id=1, source_target_pairs={{0,1},{2,3},{1,0},{3,2},{4,5},{6,7},{5,4},{7,6},{8,9},{10,11},{9,8... | collective-permute-start | bytes 221192 | tf_op jit(solution)/shard_map/ppermute | solution.py:489
  18.3 7.8 %collective-permute-start.3 = (f32[144,128]{1,0:T(8,128)S(1)}, f32[144,128]{1,0:T(8,128)S(1)}, u32[]{:S(2)}, u32[]{:S(2)}) collective-permute-start(f32[144,128]{1,0:T(8,128)S(1)} %get-tuple-element.24.z_b), channel_id=1, source_target_pairs={{1,2},{3,0},{2,1},{0,3},{5,6},{7,4},{6,5},{4,7},{9,10},{11,8},{10,... | collective-permute-start | bytes 221192 | tf_op jit(solution)/shard_map/ppermute | solution.py:489
  26.2 2.5 %shard_map.51 = (f32[24,24,128]{2,1,0:T(8,128)S(1)}, f32[2,2,3,3,12,2,128]{6,5,4,3,2,1,0:T(2,128)S(1)}) custom-call(f32[2,4,3,12,2,128]{5,4,3,2,1,0:T(2,128)S(1)} %get-tuple-element.17.s_in, f32[2,2,3,3,12,2,128]{6,5,4,3,2,1,0:T(2,128)S(1)} %get-tuple-element.18.l_in.refs_1_, f32[4,2,3,3,2,2,768]{6,5,4,3,2,1,0:T(2,128)} %links.3, ...), custom_call_target="tpu_custom_call" | custom-call | tf_op jit(solution)/shard_map/pallas_call | solution.py:470
  28.7 0.0 collective-permute-done.refs_2_.t_a
  28.7 0.0 collective-permute-done.1.refs_3_.t_b
  28.7 0.1 shard_map.52
  28.8 0.0 collective-permute-done.2.refs_2_.z_a
  28.8 1.7 %collective-permute-done.3.refs_3_.z_b = f32[144,128]{1,0:T(8,128)S(1)} collective-permute-done((f32[144,128]{1,0:T(8,128)S(1)}, f32[144,128]{1,0:T(8,128)S(1)}, u32[]{:S(2)}, u32[]{:S(2)}) %collective-permute-start.3) | collective-permute-done | bytes 73760 | tf_op jit(solution)/shard_map/ppermute | solution.py:489
  30.6 0.1 shard_map.53
  30.7 7.3 %collective-permute-start.4 = (f32[144,128]{1,0:T(8,128)S(1)}, f32[144,128]{1,0:T(8,128)S(1)}, u32[]{:S(2)}, u32[]{:S(2)}) collective-permute-start(f32[144,128]{1,0:T(8,128)S(1)} %get-tuple-element.29), channel_id=1, source_target_pairs={{0,764},{4,0},{8,4},{12,8},{16,12},{20,16},{24,20},{28,24},{32,28}... | collective-permute-start | bytes 221192 | tf_op jit(solution)/shard_map/ppermute | solution.py:483
  38.0 6.3 %collective-permute-start.5 = (f32[144,128]{1,0:T(8,128)S(1)}, f32[144,128]{1,0:T(8,128)S(1)}, u32[]{:S(2)}, u32[]{:S(2)}) collective-permute-start(f32[144,128]{1,0:T(8,128)S(1)} %get-tuple-element.30), channel_id=1, source_target_pairs={{0,3},{1,0},{2,1},{3,2},{4,7},{5,4},{6,5},{7,6},{8,11},{9,8},{10,9... | collective-permute-start | bytes 221192 | tf_op jit(solution)/shard_map/ppermute | solution.py:483
  44.3 1.8 %shard_map.54 = (f32[2,4,3,2,2,768]{5,4,3,2,1,0:T(2,128)}, f32[4,2,3,3,2,2,768]{6,5,4,3,2,1,0:T(2,128)}, f32[36,24,128]{2,1,0:T(8,128)S(1)}) custom-call(f32[2,4,3,12,2,128]{5,4,3,2,1,0:T(2,128)S(1)} %get-tuple-element.17.s_in, f32[2,4,3,12,2,128]{5,4,3,2,1,0:T(2,128)S(1)} %get-tuple-element.25.a_in, ...), custom_call_target="tpu_custom_call" | custom-call | tf_op jit(solution)/shard_map/pallas_call | solution.py:470
  46.1 0.0 collective-permute-done.4.a_t
  46.1 0.1 collective-permute-done.5.a_z
  46.2 1.2 %shard_map.55 = f32[4,2,3,3,2,2,768]{6,5,4,3,2,1,0:T(2,128)} custom-call(f32[2,4,3,12,2,128]{5,4,3,2,1,0:T(2,128)S(1)} %get-tuple-element.17.s_in, f32[2,2,3,3,12,2,128]{6,5,4,3,2,1,0:T(2,128)S(1)} %get-tuple-element.18.l_in.refs_1_, f32[36,24,128]{2,1,0:T(8,128)S(1)} %get-tuple-element.28.m_in, ...), custom_call_target="tpu_custom_call", output_to_operand_aliasing={{}: (7, {})} | custom-call | tf_op jit(solution)/shard_map/pallas_call | solution.py:470
Async XLA Ops:
  2.1 26.6 %collective-permute-start = (f32[144,128]{1,0:T(8,128)S(1)}, f32[144,128]{1,0:T(8,128)S(1)}, u32[]{:S(2)}, u32[]{:S(2)}) collective-permute-start(f32[144,128]{1,0:T(8,128)S(1)} %get-tuple-element.20), channel_id=1, source_target_pairs={{0,4},{8,12},{16,20},{24,28},{32,36},{40,44},{48,52},{56,60},{64,6... | collective-permute-start | bytes 221192 | tf_op jit(solution)/shard_map/ppermute | solution.py:489
  14.5 14.2 %collective-permute-start.1 = (f32[144,128]{1,0:T(8,128)S(1)}, f32[144,128]{1,0:T(8,128)S(1)}, u32[]{:S(2)}, u32[]{:S(2)}) collective-permute-start(f32[144,128]{1,0:T(8,128)S(1)} %get-tuple-element.21), channel_id=1, source_target_pairs={{4,8},{12,16},{20,24},{28,32},{36,40},{44,48},{52,56},{60,64},{68,... | collective-permute-start | bytes 221192 | tf_op jit(solution)/shard_map/ppermute | solution.py:489
  16.4 12.4 %collective-permute-start.2 = (f32[144,128]{1,0:T(8,128)S(1)}, f32[144,128]{1,0:T(8,128)S(1)}, u32[]{:S(2)}, u32[]{:S(2)}) collective-permute-start(f32[144,128]{1,0:T(8,128)S(1)} %get-tuple-element.23.z_a), channel_id=1, source_target_pairs={{0,1},{2,3},{1,0},{3,2},{4,5},{6,7},{5,4},{7,6},{8,9},{10,11},{9,8... | collective-permute-start | bytes 221192 | tf_op jit(solution)/shard_map/ppermute | solution.py:489
  18.3 12.2 %collective-permute-start.3 = (f32[144,128]{1,0:T(8,128)S(1)}, f32[144,128]{1,0:T(8,128)S(1)}, u32[]{:S(2)}, u32[]{:S(2)}) collective-permute-start(f32[144,128]{1,0:T(8,128)S(1)} %get-tuple-element.24.z_b), channel_id=1, source_target_pairs={{1,2},{3,0},{2,1},{0,3},{5,6},{7,4},{6,5},{4,7},{9,10},{11,8},{10,... | collective-permute-start | bytes 221192 | tf_op jit(solution)/shard_map/ppermute | solution.py:489
  30.7 15.4 %collective-permute-start.4 = (f32[144,128]{1,0:T(8,128)S(1)}, f32[144,128]{1,0:T(8,128)S(1)}, u32[]{:S(2)}, u32[]{:S(2)}) collective-permute-start(f32[144,128]{1,0:T(8,128)S(1)} %get-tuple-element.29), channel_id=1, source_target_pairs={{0,764},{4,0},{8,4},{12,8},{16,12},{20,16},{24,20},{28,24},{32,28}... | collective-permute-start | bytes 221192 | tf_op jit(solution)/shard_map/ppermute | solution.py:483
  38.0 8.3 %collective-permute-start.5 = (f32[144,128]{1,0:T(8,128)S(1)}, f32[144,128]{1,0:T(8,128)S(1)}, u32[]{:S(2)}, u32[]{:S(2)}) collective-permute-start(f32[144,128]{1,0:T(8,128)S(1)} %get-tuple-element.30), channel_id=1, source_target_pairs={{0,3},{1,0},{2,1},{3,2},{4,7},{5,4},{6,5},{7,6},{8,11},{9,8},{10,9... | collective-permute-start | bytes 221192 | tf_op jit(solution)/shard_map/ppermute | solution.py:483

commit v2 on v1

--- a/solution.py
+++ b/solution.py
@@ -9,7 +9,6 @@
 F32 = jnp.float32
 LANES = 128
 DIAG = 3.75
-PAIRED = ('ta', 'gz')
 gamma_table = (
     ((3, 0, -1), (2, 0, -1), (1, 0, 1), (0, 0, 1)),
     ((3, -1, 0), (2, 1, 0), (1, 1, 0), (0, -1, 0)),
@@ -160,27 +159,19 @@
 
 
 def outgoing(axis, up, dn):
-    if axis not in PAIRED:
-        return up, dn
     even = is_even(axis)
     return jnp.where(even, up, dn), jnp.where(even, dn, up)
 
 
 def sent_up(axis, first, second, index):
-    if axis not in PAIRED:
-        return first[index]
     return jnp.where(is_even(axis), first[index], second[index])
 
 
 def from_below(axis, first, second, index):
-    if axis not in PAIRED:
-        return first[index]
     return jnp.where(is_even(axis), second[index], first[index])
 
 
 def from_above(axis, first, second, index):
-    if axis not in PAIRED:
-        return second[index]
     return jnp.where(is_even(axis), first[index], second[index])
 
 
@@ -212,6 +203,10 @@
             ref[pl.ds(12 * (6 + 3 * s + a) + 6 * part, 6), :] = h[s][a][1]
 
 
+def get_face(ref, part):
+    return [[(ref[halo_row(3 * s + a, part)], ref[halo_row(6 + 3 * s + a, part)]) for a in range(3)] for s in range(2)]
+
+
 def face_rows(t, z):
     return pl.ds(2 * t + z, 6, stride=4)
 
@@ -221,27 +216,35 @@
 
 
 def faces_kernel(spinor, links, s_out, l_out, t_a, t_b, z_a, z_b, sem_s, sem_l):
-    copies = plane_copies(spinor, s_out, sem_s) + plane_copies(links.at[pl.ds(2, 2)], l_out, sem_l)
-    for c in copies:
+    s_copies = plane_copies(spinor, s_out, sem_s)
+    l_copies = plane_copies(links.at[pl.ds(2, 2)], l_out, sem_l)
+    for c in s_copies + l_copies:
         c.start()
     place = lax.axis_index("ta")
     up_sign = jnp.where(place == lax.axis_size("ta") - 1, -1.0, 1.0).astype(F32)
     dn_sign = jnp.where(place == 0, -1.0, 1.0).astype(F32)
-    for c in copies:
+    for c in s_copies:
         c.wait()
     s_ref, l_ref = flat(s_out), flat(l_out)
+    faces = []
     for part in range(2):
-        for axis, mu, d, first, second, low, high in (
-            ("gz", 2, 0, z_a, z_b, face_rows(part, 0), face_rows(part, 1)),
-            ("ta", 3, 1, t_a, t_b, face_rows(0, part), face_rows(1, part)),
-        ):
-            dn = half(get_spinor(s_ref, low), mu, -1)
-            up = cmul_dag(get_link(l_ref, d, high), half(get_spinor(s_ref, high), mu, 1))
-            if axis == "ta":
-                dn = hmap(lambda v: v * dn_sign, dn)
-                up = hmap(lambda v: v * up_sign, up)
-            put_face(first, part, hmap2(lambda x, y: outgoing(axis, x, y)[0], up, dn))
-            put_face(second, part, hmap2(lambda x, y: outgoing(axis, x, y)[1], up, dn))
+        faces.append(("gz", 2, z_a, z_b, part, face_rows(part, 0), face_rows(part, 1)))
+        faces.append(("ta", 3, t_a, t_b, part, face_rows(0, part), face_rows(1, part)))
+    for axis, mu, first, second, part, low, high in faces:
+        dn = half(get_spinor(s_ref, low), mu, -1)
+        if axis == "ta":
+            dn = hmap(lambda v: v * dn_sign, dn)
+        put_face(second, part, dn)
+        put_face(first, part, half(get_spinor(s_ref, high), mu, 1))
+    for c in l_copies:
+        c.wait()
+    for axis, mu, first, second, part, low, high in faces:
+        up = cmul_dag(get_link(l_ref, mu - 2, high), get_face(first, part))
+        if axis == "ta":
+            up = hmap(lambda v: v * up_sign, up)
+        dn = get_face(second, part)
+        put_face(first, part, hmap2(lambda x, y: outgoing(axis, x, y)[0], up, dn))
+        put_face(second, part, hmap2(lambda x, y: outgoing(axis, x, y)[1], up, dn))
 
 
 def local_kernel(s_in, l_in, links, clover, p_out, l_out, c_ref, chi, sem_l, sem_c):
@@ -442,16 +445,15 @@
     s_ref, l23, f = flat(s_in), flat(l_in), flat(f_ref)
     out = []
     for d, mu in ((1, 3), (0, 2)):
-        for c in range(12):
-            for k in range(3):
-                halo[c, rows_of(k), :] = jnp.zeros((8, LANES), F32)
+        low = low_rows(mu)
         if mu == 3:
             spread(halo, mu, 1, lambda c, part: a_t[halo_row(c, part)])
         else:
             spread(halo, mu, 1, lambda c, part: a_z[halo_row(c, part)] - sent_up("gz", z_a, z_b, halo_row(c, part)))
         for k in range(3):
             psi = half(get_spinor(s_ref, rows_of(k)), mu, 1)
-            m = outer(get_half(halo, rows_of(k)), psi, get_matrix(m_in, d, rows_of(k)))
+            ahead = hmap(lambda v: jnp.where(low, 0.0, v), get_half(halo, rows_of(k)))
+            m = outer(ahead, psi, get_matrix(m_in, d, rows_of(k)))
             put_force(f, d, rows_of(k), get_link(l23, d, rows_of(k)), m)
         copies = plane_copies(force.at[pl.ds(mu, 1)], f_ref.at[pl.ds(d, 1)], sem_f.at[d], out=True)
         for c in copies:
@@ -487,12 +489,6 @@
     count = lax.axis_size(axis)
     pairs = [(i % count, (i + 1) % count) for i in range(start, count + start, 2)]
     return lax.ppermute(value, axis, pairs + [(b, a) for a, b in pairs])
-
-
-def exchanged(axis, first, second):
-    if axis in PAIRED:
-        return swapped(first, axis, 0), swapped(second, axis, 1)
-    return moved(first, axis, 1), moved(second, axis, -1)
 
 
 def steps(spinor, links, clover):
@@ -511,8 +507,10 @@
         (dma, dma), (spinor, links),
     )
     z_sent = (z_a, z_b)
-    z_a, z_b = exchanged("gz", z_a, z_b)
-    t_a, t_b = exchanged("ta", t_a, t_b)
+    z_a = swapped(z_a, "gz", 0)
+    z_b = swapped(z_b, "gz", 1)
+    t_a = swapped(t_a, "ta", 0)
+    t_b = swapped(t_b, "ta", 1)
     p, l01 = call(
         local_kernel, (VMEM, VMEM, HBM, HBM), (((24,) + rows, VMEM), (l_shape, VMEM)),
         (pltpu.VMEM(c_shape, F32), halo, dma, dma), (s, l23, links, clover),

time: 47.8 us -> 47.8 us (level)
  no operation moved by 1% of the time
where the time goes in v2:
time: 47.8 us; the launch traced here: 47.5 us
  starting transfers between devices  37.6 us (79%)
  Pallas kernels  7.21 us (15%)
  waiting for transfers between devices  1.88 us (4%)
  between operations  0.74 us (2%)
    ppermute x4, starting transfers between devices, swapped(): return lax.ppermute(value, axis, pairs + [(b, a) for a, b in pairs])  24.1 us
    ppermute x2, starting transfers between devices, moved(): lax.ppermute(value, axis, [(i, (i + step) % count) for i in range(count)])  13.6 us
    pallas_call x6, Pallas kernels, call(): pl.pallas_call(kernel, out_shape=tuple((jax.ShapeDtypeStruct(shape, F32)...  7.21 us
    ppermute x4, waiting for transfers between devices, swapped(): return lax.ppermute(value, axis, pairs + [(b, a) for a, b in pairs])  1.74 us
  transfers between devices with their start and end apart: 6, of which 2 were waited for; matrix products, arithmetic and copies ran while one was open for 0% of the time, Pallas kernels for 9%

profile of v2, /device:TPU:1, one launch (start us, length us, event | category | flops | bytes accessed | tf_op | source)
XLA Modules:
  0.0 47.5 jit_solution(4242293119511618089)
XLA Ops:
  0.6 1.5 %shard_map.50 = (f32[2,4,3,12,2,128]{5,4,3,2,1,0:T(2,128)S(1)}, f32[2,2,3,3,12,2,128]{6,5,4,3,2,1,0:T(2,128)S(1)}, f32[144,128]{1,0:T(8,128)S(1)}, f32[144,128]{...) custom-call(f32[2,4,3,2,2,768]{5,4,3,2,1,0:T(2,128)} %spinor.1, f32[4,2,3,3,2,2,768]{6,5,4,3,2,1,0:T(2,128)} %links.3), custom_call_target="tpu_custom_call" | custom-call | tf_op jit(solution)/shard_map/pallas_call | solution.py:472
  2.1 12.4 %collective-permute-start = (f32[144,128]{1,0:T(8,128)S(1)}, f32[144,128]{1,0:T(8,128)S(1)}, u32[]{:S(2)}, u32[]{:S(2)}) collective-permute-start(f32[144,128]{1,0:T(8,128)S(1)} %get-tuple-element.20), channel_id=1, source_target_pairs={{0,4},{8,12},{16,20},{24,28},{32,36},{40,44},{48,52},{56,60},{64,6... | collective-permute-start | bytes 221192 | tf_op jit(solution)/shard_map/ppermute | solution.py:491
  14.5 1.9 %collective-permute-start.1 = (f32[144,128]{1,0:T(8,128)S(1)}, f32[144,128]{1,0:T(8,128)S(1)}, u32[]{:S(2)}, u32[]{:S(2)}) collective-permute-start(f32[144,128]{1,0:T(8,128)S(1)} %get-tuple-element.21), channel_id=1, source_target_pairs={{4,8},{12,16},{20,24},{28,32},{36,40},{44,48},{52,56},{60,64},{68,... | collective-permute-start | bytes 221192 | tf_op jit(solution)/shard_map/ppermute | solution.py:491
  16.4 1.9 %collective-permute-start.2 = (f32[144,128]{1,0:T(8,128)S(1)}, f32[144,128]{1,0:T(8,128)S(1)}, u32[]{:S(2)}, u32[]{:S(2)}) collective-permute-start(f32[144,128]{1,0:T(8,128)S(1)} %get-tuple-element.23.z_a), channel_id=1, source_target_pairs={{0,1},{2,3},{1,0},{3,2},{4,5},{6,7},{5,4},{7,6},{8,9},{10,11},{9,8... | collective-permute-start | bytes 221192 | tf_op jit(solution)/shard_map/ppermute | solution.py:491
  18.4 7.8 %collective-permute-start.3 = (f32[144,128]{1,0:T(8,128)S(1)}, f32[144,128]{1,0:T(8,128)S(1)}, u32[]{:S(2)}, u32[]{:S(2)}) collective-permute-start(f32[144,128]{1,0:T(8,128)S(1)} %get-tuple-element.24.z_b), channel_id=1, source_target_pairs={{1,2},{3,0},{2,1},{0,3},{5,6},{7,4},{6,5},{4,7},{9,10},{11,8},{10,... | collective-permute-start | bytes 221192 | tf_op jit(solution)/shard_map/ppermute | solution.py:491
  26.2 2.5 %shard_map.51 = (f32[24,24,128]{2,1,0:T(8,128)S(1)}, f32[2,2,3,3,12,2,128]{6,5,4,3,2,1,0:T(2,128)S(1)}) custom-call(f32[2,4,3,12,2,128]{5,4,3,2,1,0:T(2,128)S(1)} %get-tuple-element.17.s_in, f32[2,2,3,3,12,2,128]{6,5,4,3,2,1,0:T(2,128)S(1)} %get-tuple-element.18.l_in.refs_1_, f32[4,2,3,3,2,2,768]{6,5,4,3,2,1,0:T(2,128)} %links.3, ...), custom_call_target="tpu_custom_call" | custom-call | tf_op jit(solution)/shard_map/pallas_call | solution.py:472
  28.7 0.0 collective-permute-done.refs_2_.t_a
  28.7 0.0 collective-permute-done.1.refs_3_.t_b
  28.7 0.1 shard_map.52
  28.8 0.0 collective-permute-done.2.refs_2_.z_a
  28.9 1.7 %collective-permute-done.3.refs_3_.z_b = f32[144,128]{1,0:T(8,128)S(1)} collective-permute-done((f32[144,128]{1,0:T(8,128)S(1)}, f32[144,128]{1,0:T(8,128)S(1)}, u32[]{:S(2)}, u32[]{:S(2)}) %collective-permute-start.3) | collective-permute-done | bytes 73760 | tf_op jit(solution)/shard_map/ppermute | solution.py:491
  30.6 0.1 shard_map.53
  30.7 7.3 %collective-permute-start.4 = (f32[144,128]{1,0:T(8,128)S(1)}, f32[144,128]{1,0:T(8,128)S(1)}, u32[]{:S(2)}, u32[]{:S(2)}) collective-permute-start(f32[144,128]{1,0:T(8,128)S(1)} %get-tuple-element.29), channel_id=1, source_target_pairs={{0,764},{4,0},{8,4},{12,8},{16,12},{20,16},{24,20},{28,24},{32,28}... | collective-permute-start | bytes 221192 | tf_op jit(solution)/shard_map/ppermute | solution.py:485
  38.0 6.3 %collective-permute-start.5 = (f32[144,128]{1,0:T(8,128)S(1)}, f32[144,128]{1,0:T(8,128)S(1)}, u32[]{:S(2)}, u32[]{:S(2)}) collective-permute-start(f32[144,128]{1,0:T(8,128)S(1)} %get-tuple-element.30), channel_id=1, source_target_pairs={{0,3},{1,0},{2,1},{3,2},{4,7},{5,4},{6,5},{7,6},{8,11},{9,8},{10,9... | collective-permute-start | bytes 221192 | tf_op jit(solution)/shard_map/ppermute | solution.py:485
  44.3 1.8 %shard_map.54 = (f32[2,4,3,2,2,768]{5,4,3,2,1,0:T(2,128)}, f32[4,2,3,3,2,2,768]{6,5,4,3,2,1,0:T(2,128)}, f32[36,24,128]{2,1,0:T(8,128)S(1)}) custom-call(f32[2,4,3,12,2,128]{5,4,3,2,1,0:T(2,128)S(1)} %get-tuple-element.17.s_in, f32[2,4,3,12,2,128]{5,4,3,2,1,0:T(2,128)S(1)} %get-tuple-element.25.a_in, ...), custom_call_target="tpu_custom_call" | custom-call | tf_op jit(solution)/shard_map/pallas_call | solution.py:472
  46.1 0.0 collective-permute-done.4.a_t
  46.1 0.1 collective-permute-done.5.a_z
  46.2 1.2 %shard_map.55 = f32[4,2,3,3,2,2,768]{6,5,4,3,2,1,0:T(2,128)} custom-call(f32[2,4,3,12,2,128]{5,4,3,2,1,0:T(2,128)S(1)} %get-tuple-element.17.s_in, f32[2,2,3,3,12,2,128]{6,5,4,3,2,1,0:T(2,128)S(1)} %get-tuple-element.18.l_in.refs_1_, f32[36,24,128]{2,1,0:T(8,128)S(1)} %get-tuple-element.28.m_in, ...), custom_call_target="tpu_custom_call", output_to_operand_aliasing={{}: (7, {})} | custom-call | tf_op jit(solution)/shard_map/pallas_call | solution.py:472
Async XLA Ops:
  2.1 26.6 %collective-permute-start = (f32[144,128]{1,0:T(8,128)S(1)}, f32[144,128]{1,0:T(8,128)S(1)}, u32[]{:S(2)}, u32[]{:S(2)}) collective-permute-start(f32[144,128]{1,0:T(8,128)S(1)} %get-tuple-element.20), channel_id=1, source_target_pairs={{0,4},{8,12},{16,20},{24,28},{32,36},{40,44},{48,52},{56,60},{64,6... | collective-permute-start | bytes 221192 | tf_op jit(solution)/shard_map/ppermute | solution.py:491
  14.5 14.2 %collective-permute-start.1 = (f32[144,128]{1,0:T(8,128)S(1)}, f32[144,128]{1,0:T(8,128)S(1)}, u32[]{:S(2)}, u32[]{:S(2)}) collective-permute-start(f32[144,128]{1,0:T(8,128)S(1)} %get-tuple-element.21), channel_id=1, source_target_pairs={{4,8},{12,16},{20,24},{28,32},{36,40},{44,48},{52,56},{60,64},{68,... | collective-permute-start | bytes 221192 | tf_op jit(solution)/shard_map/ppermute | solution.py:491
  16.4 12.4 %collective-permute-start.2 = (f32[144,128]{1,0:T(8,128)S(1)}, f32[144,128]{1,0:T(8,128)S(1)}, u32[]{:S(2)}, u32[]{:S(2)}) collective-permute-start(f32[144,128]{1,0:T(8,128)S(1)} %get-tuple-element.23.z_a), channel_id=1, source_target_pairs={{0,1},{2,3},{1,0},{3,2},{4,5},{6,7},{5,4},{7,6},{8,9},{10,11},{9,8... | collective-permute-start | bytes 221192 | tf_op jit(solution)/shard_map/ppermute | solution.py:491
  18.4 12.2 %collective-permute-start.3 = (f32[144,128]{1,0:T(8,128)S(1)}, f32[144,128]{1,0:T(8,128)S(1)}, u32[]{:S(2)}, u32[]{:S(2)}) collective-permute-start(f32[144,128]{1,0:T(8,128)S(1)} %get-tuple-element.24.z_b), channel_id=1, source_target_pairs={{1,2},{3,0},{2,1},{0,3},{5,6},{7,4},{6,5},{4,7},{9,10},{11,8},{10,... | collective-permute-start | bytes 221192 | tf_op jit(solution)/shard_map/ppermute | solution.py:491
  30.7 15.4 %collective-permute-start.4 = (f32[144,128]{1,0:T(8,128)S(1)}, f32[144,128]{1,0:T(8,128)S(1)}, u32[]{:S(2)}, u32[]{:S(2)}) collective-permute-start(f32[144,128]{1,0:T(8,128)S(1)} %get-tuple-element.29), channel_id=1, source_target_pairs={{0,764},{4,0},{8,4},{12,8},{16,12},{20,16},{24,20},{28,24},{32,28}... | collective-permute-start | bytes 221192 | tf_op jit(solution)/shard_map/ppermute | solution.py:485
  38.0 8.3 %collective-permute-start.5 = (f32[144,128]{1,0:T(8,128)S(1)}, f32[144,128]{1,0:T(8,128)S(1)}, u32[]{:S(2)}, u32[]{:S(2)}) collective-permute-start(f32[144,128]{1,0:T(8,128)S(1)} %get-tuple-element.30), channel_id=1, source_target_pairs={{0,3},{1,0},{2,1},{3,2},{4,7},{5,4},{6,5},{7,6},{8,11},{9,8},{10,9... | collective-permute-start | bytes 221192 | tf_op jit(solution)/shard_map/ppermute | solution.py:485
